TPU v7x, 32 devices: a whole 2x2x4 slice. The times are simulated.
32 devices in a mesh: filt: 4 (over y, x), dom: 8 (over z, core).
Axes of the slice: x: 2, y: 2, z: 4, core: 2. Of those that a mesh axis runs over, the one named last changes fastest.
Arguments:
- log_weights: float32 [524288], P(('filt', 'dom')), parts along dimension 0, may hold values from -20 to 250, as said below
- bins: int32 [524288], P(('filt', 'dom')), parts along dimension 0, may hold values from 0 to 4095
- states: bfloat16 [128, 524288], P(None, ('filt', 'dom')), parts along dimension 1, may hold values from -6 to 6
Outputs:
- cumulative: float32 [16384], P(('filt', 'dom')), parts along dimension 0
- bin_means: float32 [128, 16384], P(None, ('filt', 'dom')), parts along dimension 1
- particle_weights: float32 [524288], P(('filt', 'dom')), parts along dimension 0
There are 4 independent parts, one for each index of `filt`. A program takes and returns all parts, laid end to end along the dimension named above; each array names one. Nothing has to cross between parts.
Inputs may be any that keep to these rules, and one draw needn't show every extreme that they name: `log_weights`: finite log-weights.
All inputs are finite; a program needn't handle non-finite values.
Results may differ from a plain program's by a relative error of at most 0.00051.
Values sent between devices are 32-bit elements; how exact they have to be, the bound alone decides.
A program may use at most 64 MiB of HBM per device.

v0:
```python
import functools

import jax
import jax.numpy as jnp
from jax import lax
from jax.experimental import pallas as pl
from jax.experimental.pallas import tpu as pltpu
from jax.sharding import PartitionSpec as P

BINS = 4096
LANES = 128
EXTRA = 16

floor_value = -10000.0


def spread_rows(ref, values):
    for r in range(values.shape[0]):
        ref[16 * r:16 * r + 16, :] = jnp.broadcast_to(values[r:r + 1, :], (16, LANES)).astype(ref.dtype)


def sort_pairs(keys, values):
    tile_bits = len(keys).bit_length() - 1
    bits = tile_bits + 10
    sub = lax.broadcasted_iota(jnp.int32, (8, LANES), 0)
    lane = lax.broadcasted_iota(jnp.int32, (8, LANES), 1)

    def mask_of(bit):
        if bit < tile_bits + 3:
            return (sub & (1 << (bit - tile_bits))) != 0
        return (lane & (1 << (bit - tile_bits - 3))) != 0

    def after(ka, va, kb, vb):
        return (ka > kb) | ((ka == kb) & (va > vb))

    for size in range(1, bits + 1):
        for bit in range(size - 1, -1, -1):
            down = mask_of(size) if tile_bits <= size < bits else None
            if bit < tile_bits:
                for t in range(len(keys)):
                    o = t | (1 << bit)
                    if o == t:
                        continue
                    swap = after(keys[t], values[t], keys[o], values[o])
                    if down is not None:
                        swap = jnp.logical_xor(swap, down)
                    elif size < tile_bits and t & (1 << size):
                        swap = after(keys[o], values[o], keys[t], values[t])
                    keys[t], keys[o] = jnp.where(swap, keys[o], keys[t]), jnp.where(swap, keys[t], keys[o])
                    values[t], values[o] = (jnp.where(swap, values[o], values[t]),
                                            jnp.where(swap, values[t], values[o]))
                continue
            upper = mask_of(bit)
            turn = upper if down is None else jnp.logical_xor(upper, down)
            if bit < tile_bits + 3:
                hop = 1 << (bit - tile_bits)

                def partner(x):
                    if 2 * hop == 8:
                        return pltpu.roll(x, hop, 0)
                    return jnp.where(upper, pltpu.roll(x, hop, 0), pltpu.roll(x, 8 - hop, 0))
            else:
                index = lane ^ (1 << (bit - tile_bits - 3))

                def partner(x):
                    return jnp.take_along_axis(x, index, axis=1)
            for t in range(len(keys)):
                k, v = partner(keys[t]), partner(values[t])
                swap = jnp.logical_xor(after(keys[t], values[t], k, v), turn)
                keys[t] = jnp.where(swap, k, keys[t])
                values[t] = jnp.where(swap, v, values[t])
    return keys, values


def local_tops(lw, bins):
    count = lw.shape[0] // 8
    table = BINS // LANES
    keys, values = sort_pairs([bins[8 * t:8 * t + 8] for t in range(count)],
                              [lw[8 * t:8 * t + 8] for t in range(count)])
    sub = lax.broadcasted_iota(jnp.int32, (8, LANES), 0)
    lane = lax.broadcasted_iota(jnp.int32, (8, LANES), 1)
    turned = pltpu.roll(keys[0], 7, 0)
    following = jnp.where(sub == 7, pltpu.roll(turned, LANES - 1, 1), turned)
    following = jnp.where((sub == 7) & (lane == LANES - 1), -1, following)
    high_label = lax.broadcasted_iota(jnp.int32, (table, LANES), 0)
    low_label = lax.broadcasted_iota(jnp.int32, (LANES, LANES), 0)
    found = jnp.zeros((4 * table, LANES), jnp.float32)
    for t in range(count):
        last = keys[t] != (keys[t + 1] if t + 1 < count else following)
        high = jnp.where(last, keys[t] // LANES, -1)
        low = keys[t] % LANES
        first = values[t].astype(jnp.bfloat16).astype(jnp.float32)
        rest = values[t] - first
        second = rest.astype(jnp.bfloat16).astype(jnp.float32)
        third = rest - second
        left, right = [], []
        for r in range(8):
            member = high[r:r + 1] == high_label
            pieces = [jnp.where(member, x[r:r + 1], 0.0) for x in (first, second, third)]
            pieces.append(jnp.where(member, 1.0, 0.0))
            left.append(jnp.concatenate(pieces, axis=0).astype(jnp.bfloat16))
            right.append(jnp.where(low[r:r + 1] == low_label, 1.0, 0.0).astype(jnp.bfloat16))
        found = found + lax.dot_general(jnp.concatenate(left, axis=1), jnp.concatenate(right, axis=1),
                                        (((1,), (1,)), ((), ())), preferred_element_type=jnp.float32)
    top = (found[0:table] + found[table:2 * table]) + found[2 * table:3 * table]
    return jnp.where(found[3 * table:] > 0.5, top, floor_value)


def kernel(groups, whole_count, lw_ref, bins_ref, states_ref, cum_ref, means_ref, weights_ref,
           held, ext, lo_b, hi_b, part_b, w_b, top_tab, blocks, pair_send, pair_recv, chip_send, chip_recv,
           stat_send, stat_recv, load_sem, pair_ss, pair_rs, chip_ss, chip_rs, stat_ss, stat_rs):
    state = states_ref.shape[0]
    count = states_ref.shape[1]
    rows = count // LANES
    owned = BINS // groups
    both = 2 * owned
    width = min(256, owned)
    split = both // width
    chips = groups // 2
    me = lax.axis_index("dom")
    chip, core = me // 2, me % 2
    partner = chip * 2 + (1 - core)

    load = pltpu.make_async_copy(states_ref, held, load_sem)
    load.start()
    barrier = pltpu.get_barrier_semaphore()
    for k in range(1, groups):
        pl.semaphore_signal(barrier, inc=1, device_id={"dom": lax.rem(me + k, groups)},
                            device_id_type=pl.DeviceIdType.MESH)

    lw = lw_ref[...]
    bins = bins_ref[...]
    spread_rows(lo_b, (bins % width).astype(jnp.float32))
    spread_rows(hi_b, (bins // both).astype(jnp.float32))
    spread_rows(part_b, ((bins % both) // width).astype(jnp.float32))
    tops = local_tops(lw, bins)
    low, high = bins % LANES, bins // LANES
    own_top = jnp.zeros(lw.shape, jnp.float32)
    for t in range(BINS // LANES):
        picked = jnp.take_along_axis(jnp.broadcast_to(tops[t:t + 1], lw.shape), low, axis=1)
        own_top = jnp.where(high == t, picked, own_top)
        top_tab[t] = jnp.broadcast_to(tops[t:t + 1], (8, LANES))
    spread_rows(w_b, jnp.exp(lw - own_top))
    load.wait()

    zero = jnp.zeros((), jnp.bfloat16)
    one_label = lax.broadcasted_iota(jnp.int32, (EXTRA, LANES), 0) // (EXTRA // split)
    one_label = one_label.astype(jnp.float32).astype(jnp.bfloat16)

    def mask_states(r, carry):
        part = part_b[pl.ds(pl.multiple_of(r * 16, 16), 16), :]
        cols = pl.ds(pl.multiple_of(r * LANES, LANES), LANES)
        tile = held[:, cols]
        part_all = jnp.concatenate([part] * (state // 16), axis=0)
        for q in range(split):
            ext[q * state:(q + 1) * state, cols] = jnp.where(part_all == jnp.bfloat16(q), tile, zero)
        ext[split * state:split * state + EXTRA, cols] = jnp.where(part == one_label, jnp.bfloat16(1), zero)
        return carry

    lax.fori_loop(0, rows, mask_states, 0)
    pl.semaphore_wait(barrier, groups - 1)

    depth = 16
    label = lax.broadcasted_iota(jnp.int32, (width, LANES), 0).astype(jnp.float32).astype(jnp.bfloat16)

    def block(dest, out):
        tile = dest.astype(jnp.float32).astype(jnp.bfloat16)

        def step(c, carry):
            pieces = []
            for j in range(depth):
                at = pl.ds(pl.multiple_of((c * depth + j) * 16, 16), 16)
                w = jnp.where(hi_b[at, :] == tile, w_b[at, :], zero)
                lo = lo_b[at, :]
                w_all = jnp.concatenate([w] * (width // 16), axis=0)
                lo_all = jnp.concatenate([lo] * (width // 16), axis=0)
                pieces.append(jnp.where(lo_all == label, w_all, zero))
            spread = jnp.concatenate(pieces, axis=1)
            cols = pl.ds(pl.multiple_of(c * depth * LANES, LANES), depth * LANES)
            out[...] += lax.dot_general(ext[:, cols], spread, (((1,), (1,)), ((), ())),
                                        preferred_element_type=jnp.float32)
            return carry

        out[...] = jnp.zeros(out.shape, jnp.float32)
        lax.fori_loop(0, rows // depth, step, 0)

    half = split // 2

    def part_of(found, which, p):
        sums = found[pl.ds(pl.multiple_of((which * half + p) * state, state), state), :]
        at = split * state + p * (EXTRA // split)
        first = found[at:at + 1, :]
        at = at + half * (EXTRA // split)
        return sums, jnp.where(which == 0, first, found[at:at + 1, :])

    def tops_of(owner, p):
        tiles = [top_tab[(owner * half + p) * (width // LANES) + t] for t in range(width // LANES)]
        return jnp.concatenate(tiles, axis=1)

    order = sorted(range(1, chips), key=lambda m: -min(m, chips - m)) + [0]
    pair_copies, chip_copies = [], []
    for s, m in enumerate(order):
        dest = lax.rem(chip + m, chips)
        found = blocks.at[s]
        block(dest, found)
        for p in range(half):
            lanes = slice(p * width, (p + 1) * width)
            sums, mass = part_of(found, 1 - core, p)
            pair_send[s, 0:state, lanes] = sums
            pair_send[s, state:state + 4, lanes] = jnp.broadcast_to(mass, (4, width))
            pair_send[s, state + 4:state + 8, lanes] = tops_of(dest * 2 + 1 - core, p)[0:4]
        copy = pltpu.make_async_remote_copy(
            pair_send.at[s], pair_recv.at[s], pair_ss.at[s], pair_rs.at[s],
            device_id={"dom": partner}, device_id_type=pl.DeviceIdType.MESH)
        copy.start()
        pair_copies.append(copy)
        copy.wait_recv()
        for p in range(half):
            lanes = slice(p * width, (p + 1) * width)
            sums, mass = part_of(found, core, p)
            mine = tops_of(dest * 2 + core, p)[0:4]
            theirs = pair_recv[s, state + 4:state + 8, lanes]
            top = jnp.maximum(mine, theirs)
            by_mine, by_theirs = jnp.exp(mine - top), jnp.exp(theirs - top)
            chip_send[s, 0:state, lanes] = sums * by_mine[0:1] + pair_recv[s, 0:state, lanes] * by_theirs[0:1]
            chip_send[s, state:state + 4, lanes] = mass * by_mine + pair_recv[s, state:state + 4, lanes] * by_theirs
            chip_send[s, state + 4:state + 8, lanes] = top
        if m:
            copy = pltpu.make_async_remote_copy(
                chip_send.at[s], chip_recv.at[s], chip_ss.at[s], chip_rs.at[s],
                device_id={"dom": dest * 2 + core}, device_id_type=pl.DeviceIdType.MESH)
            copy.start()
            chip_copies.append(copy)

    for copy in chip_copies:
        copy.wait_recv()
    last = chips - 1
    tops = [chip_send[last, state + 4:state + 5, :]] + [chip_recv[s, state + 4:state + 5, :] for s in range(last)]
    bin_top = functools.reduce(jnp.maximum, tops)
    sums = chip_send[last, 0:state + 8, :] * jnp.exp(tops[0] - bin_top)
    for s in range(last):
        sums = sums + chip_recv[s, 0:state + 8, :] * jnp.exp(tops[s + 1] - bin_top)
    mass = sums[state:state + 1, :]
    block_top = jnp.max(bin_top, axis=1, keepdims=True)
    block_mass = jnp.sum(mass * jnp.exp(bin_top - block_top), axis=1, keepdims=True)
    stat_send[0:4, :] = jnp.broadcast_to(block_top, (4, LANES))
    stat_send[4:8, :] = jnp.broadcast_to(block_mass, (4, LANES))
    stat_copies = []
    for k in range(1, groups):
        copy = pltpu.make_async_remote_copy(
            stat_send, stat_recv.at[k - 1], stat_ss.at[k - 1], stat_rs.at[k - 1],
            device_id={"dom": lax.rem(me + k, groups)}, device_id_type=pl.DeviceIdType.MESH)
        copy.start()
        stat_copies.append(copy)
    means_ref[...] = sums[0:state] / jnp.maximum(mass, 1.0)
    for copy in stat_copies:
        copy.wait_recv()
    top = block_top
    for k in range(groups - 1):
        top = jnp.maximum(top, stat_recv[k, 0:1, 0:1])
    total = block_mass * jnp.exp(block_top - top)
    before = jnp.zeros_like(total)
    for k in range(groups - 1):
        theirs = stat_recv[k, 4:5, 0:1] * jnp.exp(stat_recv[k, 0:1, 0:1] - top)
        total = total + theirs
        before = before + jnp.where(me >= k + 1, theirs, 0.0)
    share = mass * jnp.exp(bin_top - top)
    position = lax.broadcasted_iota(jnp.int32, share.shape, 1)
    run = share
    hop = 1
    while hop < owned:
        run = run + jnp.where(position >= hop, pltpu.roll(run, hop, 1), 0.0)
        hop *= 2
    cum_ref[...] = (before + run) / total
    weights_ref[...] = whole_count * jnp.exp(lw - top) / total
    for copy in pair_copies + chip_copies + stat_copies:
        copy.wait_send()


def body(log_weights, bins, states):
    groups = lax.axis_size("dom")
    owned = BINS // groups
    chips = groups // 2
    state, count = states.shape
    rows = count // LANES
    width = min(256, owned)
    split = 2 * owned // width
    vmem = pl.BlockSpec(memory_space=pltpu.VMEM)
    blocks = pltpu.VMEM((chips, state + 8, owned), jnp.float32)
    cumulative, bin_means, weights = pl.pallas_call(
        functools.partial(kernel, groups, float(count * groups)),
        out_shape=(jax.ShapeDtypeStruct((1, owned), jnp.float32),
                   jax.ShapeDtypeStruct((state, owned), jnp.float32),
                   jax.ShapeDtypeStruct((rows, LANES), jnp.float32)),
        in_specs=[vmem, vmem, pl.BlockSpec(memory_space=pl.ANY)],
        out_specs=(vmem, vmem, vmem),
        scratch_shapes=[
            pltpu.VMEM((state, count), jnp.bfloat16),
            pltpu.VMEM((split * state + EXTRA, count), jnp.bfloat16),
            pltpu.VMEM((rows * 16, LANES), jnp.bfloat16),
            pltpu.VMEM((rows * 16, LANES), jnp.bfloat16),
            pltpu.VMEM((rows * 16, LANES), jnp.bfloat16),
            pltpu.VMEM((rows * 16, LANES), jnp.bfloat16),
            pltpu.VMEM((BINS // LANES, 8, LANES), jnp.float32),
            pltpu.VMEM((chips, split * state + EXTRA, width), jnp.float32),
            blocks, blocks, blocks, blocks,
            pltpu.VMEM((8, LANES), jnp.float32),
            pltpu.VMEM((groups - 1, 8, LANES), jnp.float32),
            pltpu.SemaphoreType.DMA,
            pltpu.SemaphoreType.DMA((chips,)),
            pltpu.SemaphoreType.DMA((chips,)),
            pltpu.SemaphoreType.DMA((chips,)),
            pltpu.SemaphoreType.DMA((chips,)),
            pltpu.SemaphoreType.DMA((groups - 1,)),
            pltpu.SemaphoreType.DMA((groups - 1,)),
        ],
        compiler_params=pltpu.CompilerParams(
            collective_id=0, has_side_effects=True, vmem_limit_bytes=48 * 1024 * 1024),
    )(log_weights.reshape(rows, LANES), bins.reshape(rows, LANES), states)
    return cumulative.reshape(owned), bin_means, weights.reshape(count)


def solution(mesh):
    placed = (P(("filt", "dom")), P(("filt", "dom")), P(None, ("filt", "dom")))
    return jax.shard_map(
        body,
        mesh=mesh,
        in_specs=placed,
        out_specs=(P(("filt", "dom")), P(None, ("filt", "dom")), P(("filt", "dom"))),
        check_vma=False,
    )
```

profile of v0, /device:TPU:0, one launch (start us, length us, event | category | flops | bytes accessed | tf_op | source)
XLA Modules:
  0.0 58.4 jit_solution(4873651472019787522)
XLA Ops:
  0.6 0.0 copy-start
  0.6 2.2 %copy-done = bf16[128,16384]{1,0:T(8,128)(2,1)S(1)} copy-done((bf16[128,16384]{1,0:T(8,128)(2,1)S(1)}, bf16[128,16384]{1,0:T(8,128)(2,1)}, u32[]{:S(2)}) %copy-start) | copy-done | bytes 4194328
  2.8 0.0 copy-start.1
  2.8 0.8 %copy-done.1 = f32[16384]{0:T(1024)S(1)} copy-done((f32[16384]{0:T(1024)S(1)}, f32[16384]{0:T(1024)}, u32[]{:S(2)}) %copy-start.1) | copy-done | bytes 65560
  3.7 0.0 copy-start.2
  3.7 0.8 %copy-done.2 = s32[16384]{0:T(1024)S(1)} copy-done((s32[16384]{0:T(1024)S(1)}, s32[16384]{0:T(1024)}, u32[]{:S(2)}) %copy-start.2) | copy-done | bytes 65560
  4.5 52.0 %shard_map.58 = (f32[1,512]{1,0:T(1,128)S(1)}, f32[128,512]{1,0:T(8,128)S(1)}, f32[128,128]{1,0:T(8,128)S(1)}) custom-call(f32[128,128]{1,0:T(8,128)S(1)} %bitcast.4, s32[128,128]{1,0:T(8,128)S(1)} %bitcast.5, bf16[128,16384]{1,0:T(8,128)(2,1)S(1)} %copy-done), custom_call_target="tpu_custom_call" | custom-call | tf_op jit(solution)/shard_map/pallas_call | solution.py:290
  56.5 0.6 copy.9
  57.1 0.7 %copy.10 = f32[128,512]{1,0:T(8,128)} copy(f32[128,512]{1,0:T(8,128)S(1)} %get-tuple-element.13) | data formatting | bytes 524288
  57.8 0.6 %copy.11 = f32[16384]{0:T(1024)} copy(f32[16384]{0:T(1024)S(1)} %bitcast.6) | data formatting | bytes 131072
Async XLA Ops:
  0.6 2.2 %copy-start = (bf16[128,16384]{1,0:T(8,128)(2,1)S(1)}, bf16[128,16384]{1,0:T(8,128)(2,1)}, u32[]{:S(2)}) copy-start(bf16[128,16384]{1,0:T(8,128)(2,1)} %states_ref.1) | copy-start | bytes 12582916
  2.8 0.8 %copy-start.1 = (f32[16384]{0:T(1024)S(1)}, f32[16384]{0:T(1024)}, u32[]{:S(2)}) copy-start(f32[16384]{0:T(1024)} %param.3) | copy-start | bytes 196612
  3.7 0.8 %copy-start.2 = (s32[16384]{0:T(1024)S(1)}, s32[16384]{0:T(1024)}, u32[]{:S(2)}) copy-start(s32[16384]{0:T(1024)} %param.4) | copy-start | bytes 196612
where the time goes:
time: 58.7 us; the launch traced here: 58.4 us
  Pallas kernels  52 us (89%)
  local copies, waits for them, and re-layouts  5.78 us (10%)
  between operations  0.65 us (1%)
    pallas_call x1, Pallas kernels, body(): pl.pallas_call(functools.partial(kernel, groups, float(count * groups)),...  52 us
    unnamed x9, local copies, waits for them, and re-layouts  5.78 us

commit v1 on v0

--- a/solution.py
+++ b/solution.py
@@ -106,27 +106,56 @@
     return jnp.where(found[3 * table:] > 0.5, top, floor_value)
 
 
-def kernel(groups, whole_count, lw_ref, bins_ref, states_ref, cum_ref, means_ref, weights_ref,
-           held, ext, lo_b, hi_b, part_b, w_b, top_tab, blocks, pair_send, pair_recv, chip_send, chip_recv,
+def plan(chips):
+    if chips == 4:
+        order = [[3, 1, 2, 0], [2, 3, 0, 1], [1, 0, 3, 2], [0, 2, 1, 3]]
+        target = [[1, 1, 2], [2, 3, 0], [1, 0, 3], [2, 2, 1]]
+        merged = [[1, 0, 0], [0, 0, 0], [0, 0, 0], [1, 0, 0]]
+        return order, target, merged, {1: (1, 2)}, {(0, 3), (3, 0)}
+    order = [sorted((d for d in range(chips) if d != c), key=lambda d: -abs(d - c)) + [c] for c in range(chips)]
+    target = [o[:-1] for o in order]
+    merged = [[0] * (chips - 1) for _ in range(chips)]
+    return order, target, merged, {}, set()
+
+
+def pick(table, chip):
+    value = table[0]
+    for c in range(1, len(table)):
+        if table[c] != table[c - 1]:
+            value = value + jnp.where(chip >= c, table[c] - table[c - 1], 0)
+    return value
+
+
+def kernel(groups, whole_count, lw_hbm, bins_hbm, states_hbm, cum_ref, means_ref, weights_ref,
+           lw_ref, bins_ref, held, ext, lo_b, hi_b, part_b, w_b, top_tab, blocks,
+           pair_send, pair_recv, pair_send_s, pair_recv_s, send, recv, send_s, recv_s, fac, own_s,
            stat_send, stat_recv, load_sem, pair_ss, pair_rs, chip_ss, chip_rs, stat_ss, stat_rs):
-    state = states_ref.shape[0]
-    count = states_ref.shape[1]
+    state = held.shape[0]
+    count = held.shape[1]
     rows = count // LANES
     owned = BINS // groups
     both = 2 * owned
     width = min(256, owned)
     split = both // width
+    half = split // 2
+    chunks = owned // LANES
+    per = width // LANES
     chips = groups // 2
+    order, target, merged, merging, skipped = plan(chips)
     me = lax.axis_index("dom")
     chip, core = me // 2, me % 2
     partner = chip * 2 + (1 - core)
 
-    load = pltpu.make_async_copy(states_ref, held, load_sem)
-    load.start()
+    loads = [pltpu.make_async_copy(src, dst, load_sem.at[i]) for i, (src, dst) in enumerate(
+        ((lw_hbm, lw_ref), (bins_hbm, bins_ref), (states_hbm, held)))]
+    for load in loads:
+        load.start()
     barrier = pltpu.get_barrier_semaphore()
     for k in range(1, groups):
         pl.semaphore_signal(barrier, inc=1, device_id={"dom": lax.rem(me + k, groups)},
                             device_id_type=pl.DeviceIdType.MESH)
+    loads[0].wait()
+    loads[1].wait()
 
     lw = lw_ref[...]
     bins = bins_ref[...]
@@ -141,7 +170,7 @@
         own_top = jnp.where(high == t, picked, own_top)
         top_tab[t] = jnp.broadcast_to(tops[t:t + 1], (8, LANES))
     spread_rows(w_b, jnp.exp(lw - own_top))
-    load.wait()
+    loads[2].wait()
 
     zero = jnp.zeros((), jnp.bfloat16)
     one_label = lax.broadcasted_iota(jnp.int32, (EXTRA, LANES), 0) // (EXTRA // split)
@@ -160,89 +189,151 @@
     lax.fori_loop(0, rows, mask_states, 0)
     pl.semaphore_wait(barrier, groups - 1)
 
-    depth = 16
+    depth = min(64, rows) if chips <= 4 else 16
     label = lax.broadcasted_iota(jnp.int32, (width, LANES), 0).astype(jnp.float32).astype(jnp.bfloat16)
 
-    def block(dest, out):
-        tile = dest.astype(jnp.float32).astype(jnp.bfloat16)
-
-        def step(c, carry):
-            pieces = []
-            for j in range(depth):
-                at = pl.ds(pl.multiple_of((c * depth + j) * 16, 16), 16)
-                w = jnp.where(hi_b[at, :] == tile, w_b[at, :], zero)
-                lo = lo_b[at, :]
-                w_all = jnp.concatenate([w] * (width // 16), axis=0)
-                lo_all = jnp.concatenate([lo] * (width // 16), axis=0)
-                pieces.append(jnp.where(lo_all == label, w_all, zero))
-            spread = jnp.concatenate(pieces, axis=1)
-            cols = pl.ds(pl.multiple_of(c * depth * LANES, LANES), depth * LANES)
-            out[...] += lax.dot_general(ext[:, cols], spread, (((1,), (1,)), ((), ())),
-                                        preferred_element_type=jnp.float32)
+    def accumulate(dest, out, c):
+        tile = jnp.asarray(dest).astype(jnp.float32).astype(jnp.bfloat16)
+        pieces = []
+        for j in range(depth):
+            at = pl.ds(pl.multiple_of((c * depth + j) * 16, 16), 16)
+            w = jnp.where(hi_b[at, :] == tile, w_b[at, :], zero)
+            lo = lo_b[at, :]
+            w_all = jnp.concatenate([w] * (width // 16), axis=0)
+            lo_all = jnp.concatenate([lo] * (width // 16), axis=0)
+            pieces.append(jnp.where(lo_all == label, w_all, zero))
+        spread = jnp.concatenate(pieces, axis=1)
+        cols = pl.ds(pl.multiple_of(c * depth * LANES, LANES), depth * LANES)
+        out[...] += lax.dot_general(ext[:, cols], spread, (((1,), (1,)), ((), ())),
+                                    preferred_element_type=jnp.float32)
+
+    def remote(src, dst, ss, rs, chip_to, core_to):
+        return pltpu.make_async_remote_copy(src, dst, ss, rs, device_id={"dom": chip_to * 2 + core_to},
+                                            device_id_type=pl.DeviceIdType.MESH)
+
+    def sums_of(found, which, j):
+        at = pl.multiple_of((which * half + j // per) * state, state)
+        return found[pl.ds(at, state), (j % per) * LANES:(j % per + 1) * LANES]
+
+    def mass_of(found, which, j):
+        lanes = slice((j % per) * LANES, (j % per + 1) * LANES)
+        at = split * state + (j // per) * (EXTRA // split)
+        first = found[at:at + 1, lanes]
+        at = at + half * (EXTRA // split)
+        return jnp.where(which == 0, first, found[at:at + 1, lanes])
+
+    def stats_of(found, dest, which):
+        mass = [mass_of(found, which, j) for j in range(chunks)]
+        top = [top_tab[(dest * 2 + which) * chunks + j][0:1] for j in range(chunks)]
+        pad = [jnp.zeros((4 - chunks, LANES), jnp.float32)] if chunks < 4 else []
+        return jnp.concatenate(mass + pad, axis=0), jnp.concatenate(top + pad, axis=0)
+
+    def pair_copies(s):
+        return (remote(pair_send_s.at[s], pair_recv_s.at[s], pair_ss.at[0, s], pair_rs.at[0, s], chip, 1 - core),
+                remote(pair_send.at[s], pair_recv.at[s], pair_ss.at[1, s], pair_rs.at[1, s], chip, 1 - core))
+
+    def give(s, dest):
+        found = blocks.at[s % 2]
+        mass, top = stats_of(found, dest, 1 - core)
+        pair_send_s[s, 0:4] = mass
+        pair_send_s[s, 4:8] = top
+        for j in range(chunks):
+            pair_send[s, j * state:(j + 1) * state] = sums_of(found, 1 - core, j)
+        for copy in pair_copies(s):
+            copy.start()
+
+    def incoming(slot):
+        return (remote(send_s.at[0], recv_s.at[slot], chip_ss.at[0, 0], chip_rs.at[0, slot], chip, 1 - core),
+                remote(send.at[0], recv.at[slot], chip_ss.at[1, 0], chip_rs.at[1, slot], chip, 1 - core))
+
+    def outgoing(s):
+        to = pick([t[s] for t in target], chip)
+        slot = chip + pick([m[s] for m in merged], chip) * (chips - chip)
+        return (remote(send_s.at[s], recv_s.at[slot], chip_ss.at[0, s], chip_rs.at[0, slot], to, core),
+                remote(send.at[s], recv.at[slot], chip_ss.at[1, s], chip_rs.at[1, slot], to, core))
+
+    def handle(s, dest):
+        found = blocks.at[s % 2]
+        for copy in pair_copies(s):
+            copy.wait_recv()
+        mass, top = stats_of(found, dest, core)
+        theirs = pair_recv_s[s, 4:8]
+        most = jnp.maximum(top, theirs)
+        by_mine, by_theirs = jnp.exp(top - most), jnp.exp(theirs - most)
+        send_s[s, 0:4] = mass * by_mine + pair_recv_s[s, 0:4] * by_theirs
+        send_s[s, 4:8] = most
+        for j in range(chunks):
+            at = slice(j * state, (j + 1) * state)
+            send[s, at] = sums_of(found, core, j) * by_mine[j:j + 1] + pair_recv[s, at] * by_theirs[j:j + 1]
+        if s in merging:
+            first, last = merging[s]
+
+            @pl.when((chip >= first) & (chip <= last))
+            def _():
+                for copy in incoming(chips):
+                    copy.wait_recv()
+                mine, theirs = send_s[s, 4:8], recv_s[chips, 4:8]
+                most = jnp.maximum(mine, theirs)
+                by_mine, by_theirs = jnp.exp(mine - most), jnp.exp(theirs - most)
+                send_s[s, 0:4] = send_s[s, 0:4] * by_mine + recv_s[chips, 0:4] * by_theirs
+                send_s[s, 4:8] = most
+                for j in range(chunks):
+                    at = slice(j * state, (j + 1) * state)
+                    send[s, at] = send[s, at] * by_mine[j:j + 1] + recv[chips, at] * by_theirs[j:j + 1]
+        if s < chips - 1:
+            for copy in outgoing(s):
+                copy.start()
+
+    dests = [pick([o[s] for o in order], chip) for s in range(chips)]
+    for s in range(chips):
+        found = blocks.at[s % 2]
+        found[...] = jnp.zeros(found.shape, jnp.float32)
+
+        def step(c, carry, s=s, found=found):
+            accumulate(dests[s], found, c)
+            if s:
+                @pl.when(c == 0)
+                def _():
+                    handle(s - 1, dests[s - 1])
             return carry
 
-        out[...] = jnp.zeros(out.shape, jnp.float32)
         lax.fori_loop(0, rows // depth, step, 0)
-
-    half = split // 2
-
-    def part_of(found, which, p):
-        sums = found[pl.ds(pl.multiple_of((which * half + p) * state, state), state), :]
-        at = split * state + p * (EXTRA // split)
-        first = found[at:at + 1, :]
-        at = at + half * (EXTRA // split)
-        return sums, jnp.where(which == 0, first, found[at:at + 1, :])
-
-    def tops_of(owner, p):
-        tiles = [top_tab[(owner * half + p) * (width // LANES) + t] for t in range(width // LANES)]
-        return jnp.concatenate(tiles, axis=1)
-
-    order = sorted(range(1, chips), key=lambda m: -min(m, chips - m)) + [0]
-    pair_copies, chip_copies = [], []
-    for s, m in enumerate(order):
-        dest = lax.rem(chip + m, chips)
-        found = blocks.at[s]
-        block(dest, found)
-        for p in range(half):
-            lanes = slice(p * width, (p + 1) * width)
-            sums, mass = part_of(found, 1 - core, p)
-            pair_send[s, 0:state, lanes] = sums
-            pair_send[s, state:state + 4, lanes] = jnp.broadcast_to(mass, (4, width))
-            pair_send[s, state + 4:state + 8, lanes] = tops_of(dest * 2 + 1 - core, p)[0:4]
-        copy = pltpu.make_async_remote_copy(
-            pair_send.at[s], pair_recv.at[s], pair_ss.at[s], pair_rs.at[s],
-            device_id={"dom": partner}, device_id_type=pl.DeviceIdType.MESH)
-        copy.start()
-        pair_copies.append(copy)
-        copy.wait_recv()
-        for p in range(half):
-            lanes = slice(p * width, (p + 1) * width)
-            sums, mass = part_of(found, core, p)
-            mine = tops_of(dest * 2 + core, p)[0:4]
-            theirs = pair_recv[s, state + 4:state + 8, lanes]
-            top = jnp.maximum(mine, theirs)
-            by_mine, by_theirs = jnp.exp(mine - top), jnp.exp(theirs - top)
-            chip_send[s, 0:state, lanes] = sums * by_mine[0:1] + pair_recv[s, 0:state, lanes] * by_theirs[0:1]
-            chip_send[s, state:state + 4, lanes] = mass * by_mine + pair_recv[s, state:state + 4, lanes] * by_theirs
-            chip_send[s, state + 4:state + 8, lanes] = top
-        if m:
-            copy = pltpu.make_async_remote_copy(
-                chip_send.at[s], chip_recv.at[s], chip_ss.at[s], chip_rs.at[s],
-                device_id={"dom": dest * 2 + core}, device_id_type=pl.DeviceIdType.MESH)
-            copy.start()
-            chip_copies.append(copy)
-
-    for copy in chip_copies:
-        copy.wait_recv()
+        give(s, dests[s])
+
     last = chips - 1
-    tops = [chip_send[last, state + 4:state + 5, :]] + [chip_recv[s, state + 4:state + 5, :] for s in range(last)]
-    bin_top = functools.reduce(jnp.maximum, tops)
-    sums = chip_send[last, 0:state + 8, :] * jnp.exp(tops[0] - bin_top)
-    for s in range(last):
-        sums = sums + chip_recv[s, 0:state + 8, :] * jnp.exp(tops[s + 1] - bin_top)
-    mass = sums[state:state + 1, :]
-    block_top = jnp.max(bin_top, axis=1, keepdims=True)
-    block_mass = jnp.sum(mass * jnp.exp(bin_top - block_top), axis=1, keepdims=True)
+
+    def valid(sender):
+        ok = chip != sender
+        for owner, other in skipped:
+            if other == sender:
+                ok = ok & (chip != owner)
+        return ok
+
+    handle(last, dests[last])
+    for c in range(chips):
+        @pl.when(valid(c))
+        def _(c=c):
+            incoming(c)[0].wait_recv()
+
+        @pl.when(jnp.logical_not(valid(c)))
+        def _(c=c):
+            recv_s[c, 0:4] = jnp.zeros((4, LANES), jnp.float32)
+            recv_s[c, 4:8] = jnp.full((4, LANES), floor_value, jnp.float32)
+
+    own_top = send_s[last, 4:8]
+    bin_top = own_top
+    for c in range(chips):
+        bin_top = jnp.maximum(bin_top, recv_s[c, 4:8])
+    by_own = jnp.exp(own_top - bin_top)
+    mass = send_s[last, 0:4] * by_own
+    for c in range(chips):
+        by = jnp.exp(recv_s[c, 4:8] - bin_top)
+        fac[c] = by
+        mass = mass + recv_s[c, 0:4] * by
+    real = lax.broadcasted_iota(jnp.int32, (4, LANES), 0) < chunks
+    block_top = jnp.max(jnp.max(jnp.where(real, bin_top, floor_value), axis=1, keepdims=True), axis=0, keepdims=True)
+    share = jnp.where(real, mass * jnp.exp(bin_top - block_top), 0.0)
+    block_mass = jnp.sum(jnp.sum(share, axis=1, keepdims=True), axis=0, keepdims=True)
     stat_send[0:4, :] = jnp.broadcast_to(block_top, (4, LANES))
     stat_send[4:8, :] = jnp.broadcast_to(block_mass, (4, LANES))
     stat_copies = []
@@ -252,28 +343,52 @@
             device_id={"dom": lax.rem(me + k, groups)}, device_id_type=pl.DeviceIdType.MESH)
         copy.start()
         stat_copies.append(copy)
-    means_ref[...] = sums[0:state] / jnp.maximum(mass, 1.0)
+    for j in range(chunks):
+        at = slice(j * state, (j + 1) * state)
+        send[last, at] = send[last, at] * by_own[j:j + 1]
+    run = share
+    position = lax.broadcasted_iota(jnp.int32, run.shape, 1)
+    hop = 1
+    while hop < LANES:
+        run = run + jnp.where(position >= hop, pltpu.roll(run, hop, 1), 0.0)
+        hop *= 2
+    sums = [jnp.sum(share[j:j + 1], axis=1, keepdims=True) for j in range(chunks)]
+    base = jnp.zeros((1, 1), jnp.float32)
+    runs = []
+    for j in range(chunks):
+        runs.append(run[j:j + 1] + base)
+        base = base + sums[j]
     for copy in stat_copies:
         copy.wait_recv()
     top = block_top
     for k in range(groups - 1):
         top = jnp.maximum(top, stat_recv[k, 0:1, 0:1])
-    total = block_mass * jnp.exp(block_top - top)
+    scale = jnp.exp(block_top - top)
+    total = block_mass * scale
     before = jnp.zeros_like(total)
     for k in range(groups - 1):
         theirs = stat_recv[k, 4:5, 0:1] * jnp.exp(stat_recv[k, 0:1, 0:1] - top)
         total = total + theirs
         before = before + jnp.where(me >= k + 1, theirs, 0.0)
-    share = mass * jnp.exp(bin_top - top)
-    position = lax.broadcasted_iota(jnp.int32, share.shape, 1)
-    run = share
-    hop = 1
-    while hop < owned:
-        run = run + jnp.where(position >= hop, pltpu.roll(run, hop, 1), 0.0)
-        hop *= 2
-    cum_ref[...] = (before + run) / total
-    weights_ref[...] = whole_count * jnp.exp(lw - top) / total
-    for copy in pair_copies + chip_copies + stat_copies:
+    cum_ref[...] = (before + jnp.concatenate(runs, axis=1) * scale) / total
+    weights_ref[...] = whole_count * jnp.exp(lw_ref[...] - top) / total
+    for c in range(chips):
+        @pl.when(valid(c))
+        def _(c=c):
+            incoming(c)[1].wait_recv()
+            for j in range(chunks):
+                at = slice(j * state, (j + 1) * state)
+                send[last, at] = send[last, at] + recv[c, at] * fac[c, j:j + 1]
+    for j in range(chunks):
+        means_ref[:, j * LANES:(j + 1) * LANES] = (send[last, j * state:(j + 1) * state]
+                                                   / jnp.maximum(mass[j:j + 1], 1.0))
+    for s in range(chips):
+        for copy in pair_copies(s):
+            copy.wait_send()
+    for s in range(last):
+        for copy in outgoing(s):
+            copy.wait_send()
+    for copy in stat_copies:
         copy.wait_send()
 
 
@@ -285,16 +400,26 @@
     rows = count // LANES
     width = min(256, owned)
     split = 2 * owned // width
+    chunks = owned // LANES
     vmem = pl.BlockSpec(memory_space=pltpu.VMEM)
-    blocks = pltpu.VMEM((chips, state + 8, owned), jnp.float32)
+    hbm = pl.BlockSpec(memory_space=pltpu.HBM)
+
+    def sums(slots):
+        return pltpu.VMEM((slots, chunks * state, LANES), jnp.float32)
+
+    def stats(slots):
+        return pltpu.VMEM((slots, 8, LANES), jnp.float32)
+
     cumulative, bin_means, weights = pl.pallas_call(
         functools.partial(kernel, groups, float(count * groups)),
         out_shape=(jax.ShapeDtypeStruct((1, owned), jnp.float32),
                    jax.ShapeDtypeStruct((state, owned), jnp.float32),
                    jax.ShapeDtypeStruct((rows, LANES), jnp.float32)),
-        in_specs=[vmem, vmem, pl.BlockSpec(memory_space=pl.ANY)],
+        in_specs=[hbm, hbm, hbm],
         out_specs=(vmem, vmem, vmem),
         scratch_shapes=[
+            pltpu.VMEM((rows, LANES), jnp.float32),
+            pltpu.VMEM((rows, LANES), jnp.int32),
             pltpu.VMEM((state, count), jnp.bfloat16),
             pltpu.VMEM((split * state + EXTRA, count), jnp.bfloat16),
             pltpu.VMEM((rows * 16, LANES), jnp.bfloat16),
@@ -302,15 +427,18 @@
             pltpu.VMEM((rows * 16, LANES), jnp.bfloat16),
             pltpu.VMEM((rows * 16, LANES), jnp.bfloat16),
             pltpu.VMEM((BINS // LANES, 8, LANES), jnp.float32),
-            pltpu.VMEM((chips, split * state + EXTRA, width), jnp.float32),
-            blocks, blocks, blocks, blocks,
+            pltpu.VMEM((2, split * state + EXTRA, width), jnp.float32),
+            sums(chips), sums(chips), stats(chips), stats(chips),
+            sums(chips), sums(chips + 1), stats(chips), stats(chips + 1),
+            pltpu.VMEM((chips, 4, LANES), jnp.float32),
+            pltpu.VMEM((8, LANES), jnp.float32),
             pltpu.VMEM((8, LANES), jnp.float32),
             pltpu.VMEM((groups - 1, 8, LANES), jnp.float32),
-            pltpu.SemaphoreType.DMA,
-            pltpu.SemaphoreType.DMA((chips,)),
-            pltpu.SemaphoreType.DMA((chips,)),
-            pltpu.SemaphoreType.DMA((chips,)),
-            pltpu.SemaphoreType.DMA((chips,)),
+            pltpu.SemaphoreType.DMA((3,)),
+            pltpu.SemaphoreType.DMA((2, chips)),
+            pltpu.SemaphoreType.DMA((2, chips)),
+            pltpu.SemaphoreType.DMA((2, chips)),
+            pltpu.SemaphoreType.DMA((2, chips + 1)),
             pltpu.SemaphoreType.DMA((groups - 1,)),
             pltpu.SemaphoreType.DMA((groups - 1,)),
         ],

time: 58.7 us -> 51.3 us (0.87)
  Pallas kernels: 52 us -> 44.6 us
    pallas_call x1, Pallas kernels: 52 us -> 44.6 us  [body(): pl.pallas_call(functools.partial(kernel, groups, float(count * groups)),...]
where the time goes in v1:
time: 51.3 us; the launch traced here: 51 us
  Pallas kernels  44.6 us (87%)
  local copies, waits for them, and re-layouts  5.78 us (11%)
  between operations  0.65 us (1%)
    pallas_call x1, Pallas kernels, body(): pl.pallas_call(functools.partial(kernel, groups, float(count * groups)),...  44.6 us
    unnamed x9, local copies, waits for them, and re-layouts  5.78 us

profile of v1, /device:TPU:0, one launch (start us, length us, event | category | flops | bytes accessed | tf_op | source)
XLA Modules:
  0.0 51.0 jit_solution(15783482085941590053)
XLA Ops:
  0.6 0.0 copy-start
  0.6 2.2 %copy-done = bf16[128,16384]{1,0:T(8,128)(2,1)S(1)} copy-done((bf16[128,16384]{1,0:T(8,128)(2,1)S(1)}, bf16[128,16384]{1,0:T(8,128)(2,1)}, u32[]{:S(2)}) %copy-start) | copy-done | bytes 4194328
  2.8 0.0 copy-start.1
  2.8 0.8 %copy-done.1 = f32[16384]{0:T(1024)S(1)} copy-done((f32[16384]{0:T(1024)S(1)}, f32[16384]{0:T(1024)}, u32[]{:S(2)}) %copy-start.1) | copy-done | bytes 65560
  3.7 0.0 copy-start.2
  3.7 0.8 %copy-done.2 = s32[16384]{0:T(1024)S(1)} copy-done((s32[16384]{0:T(1024)S(1)}, s32[16384]{0:T(1024)}, u32[]{:S(2)}) %copy-start.2) | copy-done | bytes 65560
  4.5 44.6 %shard_map.58 = (f32[1,512]{1,0:T(1,128)S(1)}, f32[128,512]{1,0:T(8,128)S(1)}, f32[128,128]{1,0:T(8,128)S(1)}) custom-call(f32[128,128]{1,0:T(8,128)S(1)} %bitcast.4, s32[128,128]{1,0:T(8,128)S(1)} %bitcast.5, bf16[128,16384]{1,0:T(8,128)(2,1)S(1)} %copy-done), custom_call_target="tpu_custom_call" | custom-call | tf_op jit(solution)/shard_map/pallas_call | solution.py:413
  49.1 0.6 %copy.9 = f32[512]{0:T(512)} copy(f32[512]{0:T(512)S(1)} %bitcast.7) | data formatting | bytes 4096
  49.7 0.7 %copy.10 = f32[128,512]{1,0:T(8,128)} copy(f32[128,512]{1,0:T(8,128)S(1)} %get-tuple-element.13) | data formatting | bytes 524288
  50.4 0.6 %copy.11 = f32[16384]{0:T(1024)} copy(f32[16384]{0:T(1024)S(1)} %bitcast.6) | data formatting | bytes 131072
Async XLA Ops:
  0.6 2.2 %copy-start = (bf16[128,16384]{1,0:T(8,128)(2,1)S(1)}, bf16[128,16384]{1,0:T(8,128)(2,1)}, u32[]{:S(2)}) copy-start(bf16[128,16384]{1,0:T(8,128)(2,1)} %states_hbm.1) | copy-start | bytes 12582916
  2.8 0.8 %copy-start.1 = (f32[16384]{0:T(1024)S(1)}, f32[16384]{0:T(1024)}, u32[]{:S(2)}) copy-start(f32[16384]{0:T(1024)} %param.3) | copy-start | bytes 196612
  3.7 0.8 %copy-start.2 = (s32[16384]{0:T(1024)S(1)}, s32[16384]{0:T(1024)}, u32[]{:S(2)}) copy-start(s32[16384]{0:T(1024)} %param.4) | copy-start | bytes 196612

commit v2 on v1

--- a/solution.py
+++ b/solution.py
@@ -10,6 +10,10 @@
 BINS = 4096
 LANES = 128
 EXTRA = 16
+LEVEL_BITS = 20
+LEVELS = 1 << LEVEL_BITS
+LEAST = -20.0
+PER_UNIT = (LEVELS - 3) / 270.0
 
 floor_value = -10000.0
 
@@ -19,7 +23,7 @@
         ref[16 * r:16 * r + 16, :] = jnp.broadcast_to(values[r:r + 1, :], (16, LANES)).astype(ref.dtype)
 
 
-def sort_pairs(keys, values):
+def sort_keys(keys):
     tile_bits = len(keys).bit_length() - 1
     bits = tile_bits + 10
     sub = lax.broadcasted_iota(jnp.int32, (8, LANES), 0)
@@ -27,83 +31,90 @@
 
     def mask_of(bit):
         if bit < tile_bits + 3:
-            return (sub & (1 << (bit - tile_bits))) != 0
-        return (lane & (1 << (bit - tile_bits - 3))) != 0
-
-    def after(ka, va, kb, vb):
-        return (ka > kb) | ((ka == kb) & (va > vb))
-
+            return (sub >> (bit - tile_bits)) & 1
+        return (lane >> (bit - tile_bits - 3)) & 1
+
+    def turned(size):
+        if size >= bits:
+            return None
+        if size < tile_bits:
+            return [-((t >> size) & 1) for t in range(len(keys))]
+        return -mask_of(size)
+
+    def flip(now, then):
+        for t in range(len(keys)):
+            a = now[t] if isinstance(now, list) else now
+            b = then[t] if isinstance(then, list) else then
+            if a is None:
+                a = 0
+            if b is None:
+                b = 0
+            if isinstance(a, int) and isinstance(b, int):
+                if a != b:
+                    keys[t] = ~keys[t]
+                continue
+            keys[t] = keys[t] ^ (a ^ b)
+
+    before = None
     for size in range(1, bits + 1):
+        down = turned(size)
+        flip(before, down)
+        before = down
         for bit in range(size - 1, -1, -1):
-            down = mask_of(size) if tile_bits <= size < bits else None
             if bit < tile_bits:
                 for t in range(len(keys)):
                     o = t | (1 << bit)
-                    if o == t:
-                        continue
-                    swap = after(keys[t], values[t], keys[o], values[o])
-                    if down is not None:
-                        swap = jnp.logical_xor(swap, down)
-                    elif size < tile_bits and t & (1 << size):
-                        swap = after(keys[o], values[o], keys[t], values[t])
-                    keys[t], keys[o] = jnp.where(swap, keys[o], keys[t]), jnp.where(swap, keys[t], keys[o])
-                    values[t], values[o] = (jnp.where(swap, values[o], values[t]),
-                                            jnp.where(swap, values[t], values[o]))
+                    if o != t:
+                        keys[t], keys[o] = jnp.minimum(keys[t], keys[o]), jnp.maximum(keys[t], keys[o])
                 continue
-            upper = mask_of(bit)
-            turn = upper if down is None else jnp.logical_xor(upper, down)
+            upper = mask_of(bit) != 0
             if bit < tile_bits + 3:
-                hop = 1 << (bit - tile_bits)
-
-                def partner(x):
-                    if 2 * hop == 8:
-                        return pltpu.roll(x, hop, 0)
-                    return jnp.where(upper, pltpu.roll(x, hop, 0), pltpu.roll(x, 8 - hop, 0))
+                index, axis = sub ^ (1 << (bit - tile_bits)), 0
             else:
-                index = lane ^ (1 << (bit - tile_bits - 3))
-
-                def partner(x):
-                    return jnp.take_along_axis(x, index, axis=1)
+                index, axis = lane ^ (1 << (bit - tile_bits - 3)), 1
             for t in range(len(keys)):
-                k, v = partner(keys[t]), partner(values[t])
-                swap = jnp.logical_xor(after(keys[t], values[t], k, v), turn)
-                keys[t] = jnp.where(swap, k, keys[t])
-                values[t] = jnp.where(swap, v, values[t])
-    return keys, values
+                k = jnp.take_along_axis(keys[t], index, axis=axis)
+                keys[t] = jnp.where(upper, jnp.maximum(keys[t], k), jnp.minimum(keys[t], k))
+    return keys
 
 
 def local_tops(lw, bins):
     count = lw.shape[0] // 8
     table = BINS // LANES
-    keys, values = sort_pairs([bins[8 * t:8 * t + 8] for t in range(count)],
-                              [lw[8 * t:8 * t + 8] for t in range(count)])
+    level = jnp.clip((lw - LEAST) * PER_UNIT + 1.5, 1.0, float(LEVELS - 1)).astype(jnp.int32)
+    packed = (bins - BINS // 2) * LEVELS + level
+    keys = sort_keys([packed[8 * t:8 * t + 8] for t in range(count)])
     sub = lax.broadcasted_iota(jnp.int32, (8, LANES), 0)
     lane = lax.broadcasted_iota(jnp.int32, (8, LANES), 1)
-    turned = pltpu.roll(keys[0], 7, 0)
+    places = [(k >> LEVEL_BITS) + BINS // 2 for k in keys]
+    turned = pltpu.roll(places[0], 7, 0)
     following = jnp.where(sub == 7, pltpu.roll(turned, LANES - 1, 1), turned)
     following = jnp.where((sub == 7) & (lane == LANES - 1), -1, following)
-    high_label = lax.broadcasted_iota(jnp.int32, (table, LANES), 0)
-    low_label = lax.broadcasted_iota(jnp.int32, (LANES, LANES), 0)
-    found = jnp.zeros((4 * table, LANES), jnp.float32)
+    high_label = lax.broadcasted_iota(jnp.int32, (table, LANES), 0).astype(jnp.float32).astype(jnp.bfloat16)
+    low_label = lax.broadcasted_iota(jnp.int32, (LANES, LANES), 0).astype(jnp.float32).astype(jnp.bfloat16)
+    zero, one = jnp.zeros((), jnp.bfloat16), jnp.ones((), jnp.bfloat16)
+    found = jnp.zeros((3 * table, LANES), jnp.float32)
+
+    def row(x, r):
+        return jnp.broadcast_to(x[r:r + 1], (16, LANES)).astype(jnp.bfloat16)
+
     for t in range(count):
-        last = keys[t] != (keys[t + 1] if t + 1 < count else following)
-        high = jnp.where(last, keys[t] // LANES, -1)
-        low = keys[t] % LANES
-        first = values[t].astype(jnp.bfloat16).astype(jnp.float32)
-        rest = values[t] - first
-        second = rest.astype(jnp.bfloat16).astype(jnp.float32)
-        third = rest - second
+        last = places[t] != (places[t + 1] if t + 1 < count else following)
+        high = jnp.where(last, places[t] // LANES, -1).astype(jnp.float32)
+        low = (places[t] % LANES).astype(jnp.float32)
+        size = keys[t] & (LEVELS - 1)
+        parts = [(size >> 12).astype(jnp.float32), ((size >> 4) & 255).astype(jnp.float32),
+                 (size & 15).astype(jnp.float32)]
         left, right = [], []
         for r in range(8):
-            member = high[r:r + 1] == high_label
-            pieces = [jnp.where(member, x[r:r + 1], 0.0) for x in (first, second, third)]
-            pieces.append(jnp.where(member, 1.0, 0.0))
-            left.append(jnp.concatenate(pieces, axis=0).astype(jnp.bfloat16))
-            right.append(jnp.where(low[r:r + 1] == low_label, 1.0, 0.0).astype(jnp.bfloat16))
+            member = jnp.concatenate([row(high, r)] * (table // 16), axis=0) == high_label
+            left.append(jnp.concatenate(
+                [jnp.where(member, jnp.concatenate([row(x, r)] * (table // 16), axis=0), zero) for x in parts], axis=0))
+            right.append(jnp.where(jnp.concatenate([row(low, r)] * (LANES // 16), axis=0) == low_label, one, zero))
         found = found + lax.dot_general(jnp.concatenate(left, axis=1), jnp.concatenate(right, axis=1),
                                         (((1,), (1,)), ((), ())), preferred_element_type=jnp.float32)
-    top = (found[0:table] + found[table:2 * table]) + found[2 * table:3 * table]
-    return jnp.where(found[3 * table:] > 0.5, top, floor_value)
+    top = (found[0:table] * 4096.0 + found[table:2 * table] * 16.0) + found[2 * table:3 * table]
+    return jnp.where(top > 0.5, (top - 1.0) * (1.0 / PER_UNIT) + LEAST, floor_value)
 
 
 def plan(chips):
@@ -126,8 +137,8 @@
     return value
 
 
-def kernel(groups, whole_count, lw_hbm, bins_hbm, states_hbm, cum_ref, means_ref, weights_ref,
-           lw_ref, bins_ref, held, ext, lo_b, hi_b, part_b, w_b, top_tab, blocks,
+def kernel(groups, whole_count, lw_ref, bins_ref, states_hbm, cum_ref, means_ref, weights_ref,
+           held, ext, lo_b, hi_b, part_b, w_b, top_tab, blocks,
            pair_send, pair_recv, pair_send_s, pair_recv_s, send, recv, send_s, recv_s, fac, own_s,
            stat_send, stat_recv, load_sem, pair_ss, pair_rs, chip_ss, chip_rs, stat_ss, stat_rs):
     state = held.shape[0]
@@ -146,16 +157,12 @@
     chip, core = me // 2, me % 2
     partner = chip * 2 + (1 - core)
 
-    loads = [pltpu.make_async_copy(src, dst, load_sem.at[i]) for i, (src, dst) in enumerate(
-        ((lw_hbm, lw_ref), (bins_hbm, bins_ref), (states_hbm, held)))]
-    for load in loads:
-        load.start()
+    load = pltpu.make_async_copy(states_hbm, held, load_sem)
+    load.start()
     barrier = pltpu.get_barrier_semaphore()
     for k in range(1, groups):
         pl.semaphore_signal(barrier, inc=1, device_id={"dom": lax.rem(me + k, groups)},
                             device_id_type=pl.DeviceIdType.MESH)
-    loads[0].wait()
-    loads[1].wait()
 
     lw = lw_ref[...]
     bins = bins_ref[...]
@@ -170,7 +177,7 @@
         own_top = jnp.where(high == t, picked, own_top)
         top_tab[t] = jnp.broadcast_to(tops[t:t + 1], (8, LANES))
     spread_rows(w_b, jnp.exp(lw - own_top))
-    loads[2].wait()
+    load.wait()
 
     zero = jnp.zeros((), jnp.bfloat16)
     one_label = lax.broadcasted_iota(jnp.int32, (EXTRA, LANES), 0) // (EXTRA // split)
@@ -392,6 +399,15 @@
         copy.wait_send()
 
 
+def drain(*refs):
+    sources, results, sems = refs[0:3], refs[3:6], refs[6]
+    copies = [pltpu.make_async_copy(sources[i], results[i], sems.at[i]) for i in range(3)]
+    for copy in copies:
+        copy.start()
+    for copy in copies:
+        copy.wait()
+
+
 def body(log_weights, bins, states):
     groups = lax.axis_size("dom")
     owned = BINS // groups
@@ -410,16 +426,15 @@
     def stats(slots):
         return pltpu.VMEM((slots, 8, LANES), jnp.float32)
 
-    cumulative, bin_means, weights = pl.pallas_call(
+    shapes = (jax.ShapeDtypeStruct((1, owned), jnp.float32),
+              jax.ShapeDtypeStruct((state, owned), jnp.float32),
+              jax.ShapeDtypeStruct((rows, LANES), jnp.float32))
+    found = pl.pallas_call(
         functools.partial(kernel, groups, float(count * groups)),
-        out_shape=(jax.ShapeDtypeStruct((1, owned), jnp.float32),
-                   jax.ShapeDtypeStruct((state, owned), jnp.float32),
-                   jax.ShapeDtypeStruct((rows, LANES), jnp.float32)),
-        in_specs=[hbm, hbm, hbm],
+        out_shape=shapes,
+        in_specs=[vmem, vmem, hbm],
         out_specs=(vmem, vmem, vmem),
         scratch_shapes=[
-            pltpu.VMEM((rows, LANES), jnp.float32),
-            pltpu.VMEM((rows, LANES), jnp.int32),
             pltpu.VMEM((state, count), jnp.bfloat16),
             pltpu.VMEM((split * state + EXTRA, count), jnp.bfloat16),
             pltpu.VMEM((rows * 16, LANES), jnp.bfloat16),
@@ -434,7 +449,7 @@
             pltpu.VMEM((8, LANES), jnp.float32),
             pltpu.VMEM((8, LANES), jnp.float32),
             pltpu.VMEM((groups - 1, 8, LANES), jnp.float32),
-            pltpu.SemaphoreType.DMA((3,)),
+            pltpu.SemaphoreType.DMA,
             pltpu.SemaphoreType.DMA((2, chips)),
             pltpu.SemaphoreType.DMA((2, chips)),
             pltpu.SemaphoreType.DMA((2, chips)),
@@ -443,8 +458,16 @@
             pltpu.SemaphoreType.DMA((groups - 1,)),
         ],
         compiler_params=pltpu.CompilerParams(
-            collective_id=0, has_side_effects=True, vmem_limit_bytes=48 * 1024 * 1024),
+            collective_id=0, has_side_effects=True, vmem_limit_bytes=52 * 1024 * 1024),
     )(log_weights.reshape(rows, LANES), bins.reshape(rows, LANES), states)
+    cumulative, bin_means, weights = pl.pallas_call(
+        drain,
+        out_shape=shapes,
+        in_specs=[vmem, vmem, vmem],
+        out_specs=(hbm, hbm, hbm),
+        scratch_shapes=[pltpu.SemaphoreType.DMA((3,))],
+        compiler_params=pltpu.CompilerParams(vmem_limit_bytes=4 * 1024 * 1024),
+    )(*found)
     return cumulative.reshape(owned), bin_means, weights.reshape(count)
 
 

time: 51.3 us -> 46.6 us (0.908)
  local copies, waits for them, and re-layouts: 5.78 us -> 1.67 us
  Pallas kernels: 44.6 us -> 44 us
    unnamed x9 -> x4, local copies, waits for them, and re-layouts: 5.78 us -> 1.67 us
    pallas_call x1, Pallas kernels: 44.6 us -> 43.3 us  [body(): pl.pallas_call(functools.partial(kernel, groups, float(count * groups)),...]
    pallas_call x0 -> x1, Pallas kernels: none -> 0.75 us  [body(): pl.pallas_call(drain, out_shape=shapes, in_specs=[vmem, vmem, vmem], out_...]
where the time goes in v2:
time: 46.6 us; the launch traced here: 46.4 us
  Pallas kernels  44 us (94%)
  local copies, waits for them, and re-layouts  1.67 us (4%)
  between operations  0.65 us (1%)
    pallas_call x1, Pallas kernels, body(): pl.pallas_call(functools.partial(kernel, groups, float(count * groups)),...  43.3 us
    unnamed x4, local copies, waits for them, and re-layouts  1.67 us

profile of v2, /device:TPU:0, one launch (start us, length us, event | category | flops | bytes accessed | tf_op | source)
XLA Modules:
  0.0 46.4 jit_solution(4145270196845125550)
XLA Ops:
  0.6 0.0 copy-start
  0.6 0.8 %copy-done = f32[16384]{0:T(1024)S(1)} copy-done((f32[16384]{0:T(1024)S(1)}, f32[16384]{0:T(1024)}, u32[]{:S(2)}) %copy-start) | copy-done | bytes 65560
  1.5 0.0 copy-start.1
  1.5 0.8 %copy-done.1 = s32[16384]{0:T(1024)S(1)} copy-done((s32[16384]{0:T(1024)S(1)}, s32[16384]{0:T(1024)}, u32[]{:S(2)}) %copy-start.1) | copy-done | bytes 65560
  2.3 43.3 %shard_map.58 = (f32[1,512]{1,0:T(1,128)S(1)}, f32[128,512]{1,0:T(8,128)S(1)}, f32[128,128]{1,0:T(8,128)S(1)}) custom-call(f32[128,128]{1,0:T(8,128)S(1)} %bitcast.4, s32[128,128]{1,0:T(8,128)S(1)} %bitcast.5, bf16[128,16384]{1,0:T(8,128)(2,1)} %states_hbm.1), custom_call_target="tpu_custom_call" | custom-call | tf_op jit(solution)/shard_map/pallas_call | solution.py:432
  45.6 0.7 %shard_map.59 = (f32[1,512]{1,0:T(1,128)}, f32[128,512]{1,0:T(8,128)}, f32[128,128]{1,0:T(8,128)}) custom-call(f32[1,512]{1,0:T(1,128)S(1)} %get-tuple-element.9.refs_0_, f32[128,512]{1,0:T(8,128)S(1)} %get-tuple-element.10.refs_1_, f32[128,128]{1,0:T(8,128)S(1)} %get-tuple-element.11.refs_2_), custom_call_target="tpu_custom_call" | custom-call | tf_op jit(solution)/shard_map/pallas_call | solution.py:463
Async XLA Ops:
  0.6 0.8 %copy-start = (f32[16384]{0:T(1024)S(1)}, f32[16384]{0:T(1024)}, u32[]{:S(2)}) copy-start(f32[16384]{0:T(1024)} %param.3) | copy-start | bytes 196612
  1.5 0.8 %copy-start.1 = (s32[16384]{0:T(1024)S(1)}, s32[16384]{0:T(1024)}, u32[]{:S(2)}) copy-start(s32[16384]{0:T(1024)} %param.4) | copy-start | bytes 196612

commit v3 on v2

v3 whole, which is shorter than its diff:
```python
import functools

import jax
import jax.numpy as jnp
from jax import lax
from jax.experimental import pallas as pl
from jax.experimental.pallas import tpu as pltpu
from jax.sharding import PartitionSpec as P

BINS = 4096
LANES = 128
LEVEL_BITS = 20
LEVELS = 1 << LEVEL_BITS
LEAST = -20.0
PER_UNIT = (LEVELS - 3) / 270.0

floor_value = -10000.0


def spread_rows(ref, values):
    for r in range(values.shape[0]):
        ref[16 * r:16 * r + 16, :] = jnp.broadcast_to(values[r:r + 1, :], (16, LANES)).astype(ref.dtype)


def sort_keys(keys):
    tile_bits = len(keys).bit_length() - 1
    bits = tile_bits + 10
    sub = lax.broadcasted_iota(jnp.int32, (8, LANES), 0)
    lane = lax.broadcasted_iota(jnp.int32, (8, LANES), 1)

    def mask_of(bit):
        if bit < tile_bits + 3:
            return (sub >> (bit - tile_bits)) & 1
        return (lane >> (bit - tile_bits - 3)) & 1

    def turned(size):
        if size >= bits:
            return None
        if size < tile_bits:
            return [-((t >> size) & 1) for t in range(len(keys))]
        return -mask_of(size)

    def flip(now, then):
        for t in range(len(keys)):
            a = now[t] if isinstance(now, list) else now
            b = then[t] if isinstance(then, list) else then
            if a is None:
                a = 0
            if b is None:
                b = 0
            if isinstance(a, int) and isinstance(b, int):
                if a != b:
                    keys[t] = ~keys[t]
                continue
            keys[t] = keys[t] ^ (a ^ b)

    before = None
    for size in range(1, bits + 1):
        down = turned(size)
        flip(before, down)
        before = down
        for bit in range(size - 1, -1, -1):
            if bit < tile_bits:
                for t in range(len(keys)):
                    o = t | (1 << bit)
                    if o != t:
                        keys[t], keys[o] = jnp.minimum(keys[t], keys[o]), jnp.maximum(keys[t], keys[o])
                continue
            upper = mask_of(bit) != 0
            if bit < tile_bits + 3:
                index, axis = sub ^ (1 << (bit - tile_bits)), 0
            else:
                index, axis = lane ^ (1 << (bit - tile_bits - 3)), 1
            for t in range(len(keys)):
                k = jnp.take_along_axis(keys[t], index, axis=axis)
                keys[t] = jnp.where(upper, jnp.maximum(keys[t], k), jnp.minimum(keys[t], k))
    return keys


def local_tops(lw, bins):
    count = lw.shape[0] // 8
    table = BINS // LANES
    level = jnp.clip((lw - LEAST) * PER_UNIT + 1.5, 1.0, float(LEVELS - 1)).astype(jnp.int32)
    packed = (bins - BINS // 2) * LEVELS + level
    keys = sort_keys([packed[8 * t:8 * t + 8] for t in range(count)])
    sub = lax.broadcasted_iota(jnp.int32, (8, LANES), 0)
    lane = lax.broadcasted_iota(jnp.int32, (8, LANES), 1)
    places = [(k >> LEVEL_BITS) + BINS // 2 for k in keys]
    turned = pltpu.roll(places[0], 7, 0)
    following = jnp.where(sub == 7, pltpu.roll(turned, LANES - 1, 1), turned)
    following = jnp.where((sub == 7) & (lane == LANES - 1), -1, following)
    high_label = lax.broadcasted_iota(jnp.int32, (table, LANES), 0).astype(jnp.float32).astype(jnp.bfloat16)
    low_label = lax.broadcasted_iota(jnp.int32, (LANES, LANES), 0).astype(jnp.float32).astype(jnp.bfloat16)
    zero, one = jnp.zeros((), jnp.bfloat16), jnp.ones((), jnp.bfloat16)
    found = jnp.zeros((3 * table, LANES), jnp.float32)

    def row(x, r):
        return jnp.broadcast_to(x[r:r + 1], (16, LANES)).astype(jnp.bfloat16)

    for t in range(count):
        last = places[t] != (places[t + 1] if t + 1 < count else following)
        high = jnp.where(last, places[t] // LANES, -1).astype(jnp.float32)
        low = (places[t] % LANES).astype(jnp.float32)
        size = keys[t] & (LEVELS - 1)
        parts = [(size >> 12).astype(jnp.float32), ((size >> 4) & 255).astype(jnp.float32),
                 (size & 15).astype(jnp.float32)]
        left, right = [], []
        for r in range(8):
            member = jnp.concatenate([row(high, r)] * (table // 16), axis=0) == high_label
            left.append(jnp.concatenate(
                [jnp.where(member, jnp.concatenate([row(x, r)] * (table // 16), axis=0), zero) for x in parts], axis=0))
            right.append(jnp.where(jnp.concatenate([row(low, r)] * (LANES // 16), axis=0) == low_label, one, zero))
        found = found + lax.dot_general(jnp.concatenate(left, axis=1), jnp.concatenate(right, axis=1),
                                        (((1,), (1,)), ((), ())), preferred_element_type=jnp.float32)
    top = (found[0:table] * 4096.0 + found[table:2 * table] * 16.0) + found[2 * table:3 * table]
    return jnp.where(top > 0.5, (top - 1.0) * (1.0 / PER_UNIT) + LEAST, floor_value)


def plan(chips):
    if chips == 4:
        order = [[3, 1, 2, 0], [2, 3, 0, 1], [1, 0, 3, 2], [0, 2, 1, 3]]
        target = [[1, 1, 2], [2, 3, 0], [1, 0, 3], [2, 2, 1]]
        merged = [[1, 0, 0], [0, 0, 0], [0, 0, 0], [1, 0, 0]]
        return order, target, merged, {1: (1, 2)}, {(0, 3), (3, 0)}
    order = [sorted((d for d in range(chips) if d != c), key=lambda d: -abs(d - c)) + [c] for c in range(chips)]
    target = [o[:-1] for o in order]
    merged = [[0] * (chips - 1) for _ in range(chips)]
    return order, target, merged, {}, set()


def pick(table, chip):
    value = table[0]
    for c in range(1, len(table)):
        if table[c] != table[c - 1]:
            value = value + jnp.where(chip >= c, table[c] - table[c - 1], 0)
    return value


def kernel(groups, whole_count, lw_ref, bins_ref, states_hbm, cum_ref, means_ref, weights_ref,
           held, ext, lo_b, hi_b, part_b, w_b, top_tab, mass_tab, blocks,
           tops_send, tops_recv, mass_send, mass_recv, pair_send, pair_recv, by_mine, by_theirs,
           send, recv, send_s, recv_s, fac, stat_send, stat_recv,
           load_sem, table_ss, table_rs, pair_ss, pair_rs, chip_ss, chip_rs, word_ss, word_rs, stat_ss, stat_rs):
    state = held.shape[0]
    count = held.shape[1]
    rows = count // LANES
    owned = BINS // groups
    both = 2 * owned
    width = min(256, owned)
    half = owned // width
    chunks = owned // LANES
    per = width // LANES
    chips = groups // 2
    units = chips * half
    last = chips - 1
    order, target, merged, merging, skipped = plan(chips)
    me = lax.axis_index("dom")
    chip, core = me // 2, me % 2
    dests = [pick([o[s] for o in order], chip) for s in range(chips)]

    load = pltpu.make_async_copy(states_hbm, held, load_sem)
    load.start()
    barrier = pltpu.get_barrier_semaphore()
    for k in range(1, groups):
        pl.semaphore_signal(barrier, inc=1, device_id={"dom": lax.rem(me + k, groups)},
                            device_id_type=pl.DeviceIdType.MESH)

    lw = lw_ref[...]
    bins = bins_ref[...]
    spread_rows(lo_b, (bins % width).astype(jnp.float32))
    spread_rows(hi_b, (bins // both).astype(jnp.float32))
    spread_rows(part_b, ((bins % both) // width).astype(jnp.float32))
    tops = local_tops(lw, bins)
    low, high = bins % LANES, bins // LANES
    own_top = jnp.zeros(lw.shape, jnp.float32)
    for t in range(BINS // LANES):
        picked = jnp.take_along_axis(jnp.broadcast_to(tops[t:t + 1], lw.shape), low, axis=1)
        own_top = jnp.where(high == t, picked, own_top)
        top_tab[t] = jnp.broadcast_to(tops[t:t + 1], (8, LANES))
    spread_rows(w_b, jnp.exp(lw - own_top))
    load.wait()

    zero = jnp.zeros((), jnp.bfloat16)

    def mask_states(p):
        def step(r, carry):
            part = part_b[pl.ds(pl.multiple_of(r * 16, 16), 16), :]
            cols = pl.ds(pl.multiple_of(r * LANES, LANES), LANES)
            tile = held[:, cols]
            part_all = jnp.concatenate([part] * (state // 16), axis=0)
            for k in range(2):
                at = (2 * p + k) * state
                ext[at:at + state, cols] = jnp.where(part_all == jnp.bfloat16(k * half + p), tile, zero)
            return carry

        lax.fori_loop(0, rows, step, 0)

    label = lax.broadcasted_iota(jnp.int32, (width, LANES), 0).astype(jnp.float32).astype(jnp.bfloat16)

    def product(dest, p, c, depth):
        tile = jnp.asarray(dest).astype(jnp.float32).astype(jnp.bfloat16)
        pieces = []
        for j in range(depth):
            at = pl.ds(pl.multiple_of((c * depth + j) * 16, 16), 16)
            w = jnp.where(hi_b[at, :] == tile, w_b[at, :], zero)
            lo = lo_b[at, :]
            w_all = jnp.concatenate([w] * (width // 16), axis=0)
            lo_all = jnp.concatenate([lo] * (width // 16), axis=0)
            pieces.append(jnp.where(lo_all == label, w_all, zero))
        spread = jnp.concatenate(pieces, axis=1)
        cols = pl.ds(pl.multiple_of(c * depth * LANES, LANES), depth * LANES)
        left = ext[pl.ds(pl.multiple_of(2 * p * state, 2 * state), 2 * state), cols]
        return lax.dot_general(left, spread, (((1,), (1,)), ((), ())), preferred_element_type=jnp.float32)

    def mass_table():
        side = 64
        depth = min(32, rows)
        per_row = BINS // side
        low_label = lax.broadcasted_iota(jnp.int32, (side, LANES), 0).astype(jnp.float32).astype(jnp.bfloat16)
        turn = lax.broadcasted_iota(jnp.int32, (per_row, LANES), 0)
        turn = 2 * (turn % (per_row // 2)) + turn // (per_row // 2)
        high_label = turn.astype(jnp.float32).astype(jnp.bfloat16)
        one = jnp.ones((), jnp.bfloat16)

        def step(c, carry):
            left, right = [], []
            for j in range(depth):
                at = pl.ds(pl.multiple_of((c * depth + j) * 16, 16), 16)
                lo = lo_b[at, :]
                high = hi_b[at, :] * jnp.bfloat16(both // side) + part_b[at, :] * jnp.bfloat16(width // side)
                step = width // 2
                while step >= side:
                    over = lo >= jnp.bfloat16(step)
                    lo = jnp.where(over, lo - jnp.bfloat16(step), lo)
                    high = jnp.where(over, high + jnp.bfloat16(step // side), high)
                    step //= 2
                w = w_b[at, :]
                left.append(jnp.where(jnp.concatenate([high] * (per_row // 16), axis=0) == high_label,
                                      jnp.concatenate([w] * (per_row // 16), axis=0), zero))
                right.append(jnp.where(jnp.concatenate([lo] * (side // 16), axis=0) == low_label, one, zero))
            return carry + lax.dot_general(jnp.concatenate(left, axis=1), jnp.concatenate(right, axis=1),
                                           (((1,), (1,)), ((), ())), preferred_element_type=jnp.float32)

        found = lax.fori_loop(0, rows // depth, step, jnp.zeros((per_row, side), jnp.float32))
        found = jnp.concatenate([found[0:per_row // 2], found[per_row // 2:]], axis=1)
        for t in range(BINS // LANES):
            mass_tab[t] = jnp.broadcast_to(found[t:t + 1], (8, LANES))

    def remote(src, dst, ss, rs, chip_to, core_to):
        return pltpu.make_async_remote_copy(src, dst, ss, rs, device_id={"dom": chip_to * 2 + core_to},
                                            device_id_type=pl.DeviceIdType.MESH)

    def rows_of(table, dest, which):
        found = [table[(dest * 2 + which) * chunks + j][0:1] for j in range(chunks)]
        pad = [jnp.zeros((4 - chunks, LANES), jnp.float32)] if chunks < 4 else []
        return jnp.concatenate(found + pad, axis=0)

    def table_copy(which):
        src, dst = ((tops_send, tops_recv), (mass_send, mass_recv))[which]
        return remote(src, dst, table_ss.at[which], table_rs.at[which], chip, 1 - core)

    def pair_copy(u):
        return remote(pair_send.at[u], pair_recv.at[u], pair_ss.at[u], pair_rs.at[u], chip, 1 - core)

    def piece(p):
        return pl.ds(pl.multiple_of(p * per * state, per * state), per * state)

    def chunk(j):
        return pl.ds(pl.multiple_of(j * state, state), state)

    def incoming(slot, p):
        return remote(send.at[0, piece(p)], recv.at[slot, piece(p)], chip_ss.at[0], chip_rs.at[slot, p], chip, 1 - core)

    def incoming_word(slot):
        return remote(send_s.at[0], recv_s.at[slot], word_ss.at[0], word_rs.at[slot], chip, 1 - core)

    def at_step(values, s):
        found = values[0]
        for k in range(1, len(values)):
            found = found + jnp.where(s == k, values[k] - values[0], 0)
        return found

    targets = [pick([t[s] for t in target], chip) for s in range(last)]
    slots = [chip + pick([m[s] for m in merged], chip) * (chips - chip) for s in range(last)]

    def outgoing(u):
        s, p = u // half, u % half
        return remote(send.at[s, piece(p)], recv.at[at_step(slots, s), piece(p)], chip_ss.at[u],
                      chip_rs.at[at_step(slots, s), p], at_step(targets, s), core)

    def outgoing_word(s):
        return remote(send_s.at[s], recv_s.at[slots[s]], word_ss.at[s], word_rs.at[slots[s]], targets[s], core)

    def merges(s):
        first, final = merging[s]
        return (chip >= first) & (chip <= final)

    def give(u):
        found = blocks[u % 2, pl.ds(pl.multiple_of((1 - core) * state, state), state)]
        for l in range(per):
            pair_send[u, l * state:(l + 1) * state] = found[:, l * LANES:(l + 1) * LANES]
        pair_copy(u).start()

    def keep(table, s, values):
        for j in range(chunks):
            table[s * chunks + j] = jnp.broadcast_to(values[j:j + 1], (8, LANES))

    def handle_tops():
        table_copy(0).wait_recv()
        for s in range(chips):
            mine, theirs = rows_of(top_tab, dests[s], core), tops_recv[s]
            most = jnp.maximum(mine, theirs)
            keep(by_mine, s, jnp.exp(mine - most))
            keep(by_theirs, s, jnp.exp(theirs - most))
            send_s[s, 4:8] = most

    def handle_masses():
        table_copy(1).wait_recv()
        for s in range(chips):
            for j in range(chunks):
                mine = mass_tab[(dests[s] * 2 + core) * chunks + j][0:1]
                send_s[s, j:j + 1] = (mine * by_mine[s * chunks + j, 0:1]
                                      + mass_recv[s, j:j + 1] * by_theirs[s * chunks + j, 0:1])
            for j in range(chunks, 4):
                send_s[s, j:j + 1] = jnp.zeros((1, LANES), jnp.float32)
            if s < last and s not in merging:
                outgoing_word(s).start()

    def scale_step(s, values):
        for j in range(chunks):
            by_mine[s * chunks + j] = by_mine[s * chunks + j] * values[j:j + 1]
            by_theirs[s * chunks + j] = by_theirs[s * chunks + j] * values[j:j + 1]

    def merge_words(s):
        @pl.when(merges(s))
        def _():
            incoming_word(chips).wait_recv()
            mine, theirs = send_s[s, 4:8], recv_s[chips, 4:8]
            most = jnp.maximum(mine, theirs)
            to_mine, to_theirs = jnp.exp(mine - most), jnp.exp(theirs - most)
            scale_step(s, to_mine)
            keep(fac, chips, to_theirs)
            send_s[s, 0:4] = send_s[s, 0:4] * to_mine + recv_s[chips, 0:4] * to_theirs
            send_s[s, 4:8] = most

        outgoing_word(s).start()

    def handle(u):
        s, p = u // half, u % half
        for m in merging:
            @pl.when(u == m * half)
            def _(m=m):
                merge_words(m)
        pair_copy(u).wait_recv()
        found = blocks[u % 2, pl.ds(pl.multiple_of(core * state, state), state)]
        for l in range(per):
            j = p * per + l
            send[s, chunk(j)] = (
                found[:, l * LANES:(l + 1) * LANES] * by_mine[s * chunks + j, 0:1]
                + pair_recv[u, l * state:(l + 1) * state] * by_theirs[s * chunks + j, 0:1])
        for m in merging:
            @pl.when((s == m) & merges(m))
            def _(m=m):
                incoming(chips, p).wait_recv()
                for l in range(per):
                    j = p * per + l
                    send[m, chunk(j)] = send[m, chunk(j)] + recv[chips, chunk(j)] * fac[chips * chunks + j, 0:1]

        @pl.when(s < last)
        def _():
            outgoing(u).start()

    def valid(sender):
        ok = chip != sender
        for owner, other in skipped:
            if other == sender:
                ok = ok & (chip != owner)
        return ok

    real = lax.broadcasted_iota(jnp.int32, (4, LANES), 0) < chunks

    def stat_copies():
        return [pltpu.make_async_remote_copy(
            stat_send, stat_recv.at[k - 1], stat_ss.at[k - 1], stat_rs.at[k - 1],
            device_id={"dom": lax.rem(me + k, groups)}, device_id_type=pl.DeviceIdType.MESH)
            for k in range(1, groups)]

    def owned_words():
        for c in range(chips):
            @pl.when(valid(c))
            def _(c=c):
                incoming_word(c).wait_recv()

            @pl.when(jnp.logical_not(valid(c)))
            def _(c=c):
                recv_s[c, 0:4] = jnp.zeros((4, LANES), jnp.float32)
                recv_s[c, 4:8] = jnp.full((4, LANES), floor_value, jnp.float32)

        own = send_s[last, 4:8]
        bin_top = own
        for c in range(chips):
            bin_top = jnp.maximum(bin_top, recv_s[c, 4:8])
        by_own = jnp.exp(own - bin_top)
        mass = send_s[last, 0:4] * by_own
        for c in range(chips):
            by = jnp.exp(recv_s[c, 4:8] - bin_top)
            keep(fac, c, by)
            mass = mass + recv_s[c, 0:4] * by
        scale_step(last, by_own)
        block_top = jnp.max(jnp.max(jnp.where(real, bin_top, floor_value), axis=1, keepdims=True), axis=0,
                            keepdims=True)
        share = jnp.where(real, mass * jnp.exp(bin_top - block_top), 0.0)
        block_mass = jnp.sum(jnp.sum(share, axis=1, keepdims=True), axis=0, keepdims=True)
        send_s[last, 0:4] = mass
        send_s[last, 4:8] = share
        stat_send[0:4, :] = jnp.broadcast_to(block_top, (4, LANES))
        stat_send[4:8, :] = jnp.broadcast_to(block_mass, (4, LANES))
        for copy in stat_copies():
            copy.start()

    def close_stats():
        share = send_s[last, 4:8]
        run = share
        position = lax.broadcasted_iota(jnp.int32, run.shape, 1)
        hop = 1
        while hop < LANES:
            run = run + jnp.where(position >= hop, pltpu.roll(run, hop, 1), 0.0)
            hop *= 2
        base = jnp.zeros((1, 1), jnp.float32)
        runs = []
        for j in range(chunks):
            runs.append(run[j:j + 1] + base)
            base = base + run[j:j + 1, LANES - 1:LANES]
        for copy in stat_copies():
            copy.wait_recv()
        block_top, block_mass = stat_send[0:1, 0:1], stat_send[4:5, 0:1]
        top = block_top
        for k in range(groups - 1):
            top = jnp.maximum(top, stat_recv[k, 0:1, 0:1])
        scale = jnp.exp(block_top - top)
        total = block_mass * scale
        before = jnp.zeros_like(total)
        for k in range(groups - 1):
            theirs = stat_recv[k, 4:5, 0:1] * jnp.exp(stat_recv[k, 0:1, 0:1] - top)
            total = total + theirs
            before = before + jnp.where(me >= k + 1, theirs, 0.0)
        cum_ref[...] = (before + jnp.concatenate(runs, axis=1) * scale) / total
        weights_ref[...] = whole_count * jnp.exp(lw_ref[...] - top) / total

    for s in range(chips):
        tops_send[s] = rows_of(top_tab, dests[s], 1 - core)
    mask_states(0)
    pl.semaphore_wait(barrier, groups - 1)
    table_copy(0).start()
    depth = min(64, rows) if chips <= 4 else min(16, rows)
    steps = rows // depth

    def turn(v, carry):
        u, c = v // steps, v % steps
        s, p = u // half, u % half
        found = blocks.at[u % 2]
        added = product(at_step(dests, s), p, c, depth)

        found[...] = jnp.where(c > 0, found[...], 0.0) + added

        @pl.when(v == 2 * steps - 1)
        def _():
            handle_masses()

        @pl.when(v == (units - 1) * steps)
        def _():
            owned_words()

        @pl.when((c == 0) & (u > 1))
        def _():
            handle(u - 1)

        @pl.when(c == steps - 1)
        def _():
            give(u)

        @pl.when(v == steps - 1)
        def _():
            for q in range(1, half):
                mask_states(q)
            mass_table()
            for t in range(chips):
                mass_send[t] = rows_of(mass_tab, dests[t], 1 - core)
            table_copy(1).start()
            handle_tops()
            handle(0)

        return carry

    lax.fori_loop(0, units * steps, turn, 0)
    handle(units - 1)
    close_stats()
    for c in range(chips):
        @pl.when(valid(c))
        def _(c=c):
            for p in range(half):
                incoming(c, p).wait_recv()
            for j in range(chunks):
                at = slice(j * state, (j + 1) * state)
                send[last, at] = send[last, at] + recv[c, at] * fac[c * chunks + j, 0:1]
    for j in range(chunks):
        means_ref[:, j * LANES:(j + 1) * LANES] = (send[last, j * state:(j + 1) * state]
                                                   / jnp.maximum(send_s[last, j:j + 1], 1.0))
    for which in range(2):
        table_copy(which).wait_send()
    for u in range(units):
        pair_copy(u).wait_send()
    for u in range(last * half):
        outgoing(u).wait_send()
    for s in range(last):
        outgoing_word(s).wait_send()
    for copy in stat_copies():
        copy.wait_send()


def drain(*refs):
    sources, results, sems = refs[0:3], refs[3:6], refs[6]
    copies = [pltpu.make_async_copy(sources[i], results[i], sems.at[i]) for i in range(3)]
    for copy in copies:
        copy.start()
    for copy in copies:
        copy.wait()


def body(log_weights, bins, states):
    groups = lax.axis_size("dom")
    owned = BINS // groups
    chips = groups // 2
    state, count = states.shape
    rows = count // LANES
    width = min(256, owned)
    chunks = owned // LANES
    vmem = pl.BlockSpec(memory_space=pltpu.VMEM)
    hbm = pl.BlockSpec(memory_space=pltpu.HBM)

    half = owned // width
    units = chips * half

    def sums(slots):
        return pltpu.VMEM((slots, chunks * state, LANES), jnp.float32)

    def words(slots, depth=8):
        return pltpu.VMEM((slots, depth, LANES), jnp.float32)

    def spread():
        return pltpu.VMEM((rows * 16, LANES), jnp.bfloat16)

    shapes = (jax.ShapeDtypeStruct((1, owned), jnp.float32),
              jax.ShapeDtypeStruct((state, owned), jnp.float32),
              jax.ShapeDtypeStruct((rows, LANES), jnp.float32))
    found = pl.pallas_call(
        functools.partial(kernel, groups, float(count * groups)),
        out_shape=shapes,
        in_specs=[vmem, vmem, hbm],
        out_specs=(vmem, vmem, vmem),
        scratch_shapes=[
            pltpu.VMEM((state, count), jnp.bfloat16),
            pltpu.VMEM((2 * half * state, count), jnp.bfloat16),
            spread(), spread(), spread(), spread(),
            words(BINS // LANES), words(BINS // LANES),
            pltpu.VMEM((2, 2 * state, width), jnp.float32),
            words(chips, 4), words(chips, 4), words(chips, 4), words(chips, 4),
            pltpu.VMEM((units, (width // LANES) * state, LANES), jnp.float32),
            pltpu.VMEM((units, (width // LANES) * state, LANES), jnp.float32),
            words(chips * chunks), words(chips * chunks),
            sums(chips), sums(chips + 1), words(chips), words(chips + 1), words((chips + 1) * chunks),
            pltpu.VMEM((8, LANES), jnp.float32),
            words(groups - 1),
            pltpu.SemaphoreType.DMA,
            pltpu.SemaphoreType.DMA((2,)),
            pltpu.SemaphoreType.DMA((2,)),
            pltpu.SemaphoreType.DMA((units,)),
            pltpu.SemaphoreType.DMA((units,)),
            pltpu.SemaphoreType.DMA((units,)),
            pltpu.SemaphoreType.DMA((chips + 1, half)),
            pltpu.SemaphoreType.DMA((chips,)),
            pltpu.SemaphoreType.DMA((chips + 1,)),
            pltpu.SemaphoreType.DMA((groups - 1,)),
            pltpu.SemaphoreType.DMA((groups - 1,)),
        ],
        compiler_params=pltpu.CompilerParams(
            collective_id=0, has_side_effects=True, vmem_limit_bytes=52 * 1024 * 1024),
    )(log_weights.reshape(rows, LANES), bins.reshape(rows, LANES), states)
    cumulative, bin_means, weights = pl.pallas_call(
        drain,
        out_shape=shapes,
        in_specs=[vmem, vmem, vmem],
        out_specs=(hbm, hbm, hbm),
        scratch_shapes=[pltpu.SemaphoreType.DMA((3,))],
        compiler_params=pltpu.CompilerParams(vmem_limit_bytes=4 * 1024 * 1024),
    )(*found)
    return cumulative.reshape(owned), bin_means, weights.reshape(count)


def solution(mesh):
    placed = (P(("filt", "dom")), P(("filt", "dom")), P(None, ("filt", "dom")))
    return jax.shard_map(
        body,
        mesh=mesh,
        in_specs=placed,
        out_specs=(P(("filt", "dom")), P(None, ("filt", "dom")), P(("filt", "dom"))),
        check_vma=False,
    )
```

time: 46.6 us -> 44.3 us (0.951)
  Pallas kernels: 44 us -> 41.8 us
    pallas_call x1, Pallas kernels: 43.3 us -> 41 us  [body(): pl.pallas_call(functools.partial(kernel, groups, float(count * groups)),...]
where the time goes in v3:
time: 44.3 us; the launch traced here: 44.1 us
  Pallas kernels  41.8 us (94%)
  local copies, waits for them, and re-layouts  1.67 us (4%)
  between operations  0.65 us (1%)
    pallas_call x1, Pallas kernels, body(): pl.pallas_call(functools.partial(kernel, groups, float(count * groups)),...  41 us
    unnamed x4, local copies, waits for them, and re-layouts  1.67 us

profile of v3, /device:TPU:0, one launch (start us, length us, event | category | flops | bytes accessed | tf_op | source)
XLA Modules:
  0.0 44.1 jit_solution(16473598748360184909)
XLA Ops:
  0.6 0.0 copy-start
  0.6 0.8 %copy-done = f32[16384]{0:T(1024)S(1)} copy-done((f32[16384]{0:T(1024)S(1)}, f32[16384]{0:T(1024)}, u32[]{:S(2)}) %copy-start) | copy-done | bytes 65560
  1.5 0.0 copy-start.1
  1.5 0.8 %copy-done.1 = s32[16384]{0:T(1024)S(1)} copy-done((s32[16384]{0:T(1024)S(1)}, s32[16384]{0:T(1024)}, u32[]{:S(2)}) %copy-start.1) | copy-done | bytes 65560
  2.3 41.0 %shard_map.58 = (f32[1,512]{1,0:T(1,128)S(1)}, f32[128,512]{1,0:T(8,128)S(1)}, f32[128,128]{1,0:T(8,128)S(1)}) custom-call(f32[128,128]{1,0:T(8,128)S(1)} %bitcast.4, s32[128,128]{1,0:T(8,128)S(1)} %bitcast.5, bf16[128,16384]{1,0:T(8,128)(2,1)} %states_hbm.1), custom_call_target="tpu_custom_call" | custom-call | tf_op jit(solution)/shard_map/pallas_call | solution.py:556
  43.3 0.7 %shard_map.59 = (f32[1,512]{1,0:T(1,128)}, f32[128,512]{1,0:T(8,128)}, f32[128,128]{1,0:T(8,128)}) custom-call(f32[1,512]{1,0:T(1,128)S(1)} %get-tuple-element.9.refs_0_, f32[128,512]{1,0:T(8,128)S(1)} %get-tuple-element.10.refs_1_, f32[128,128]{1,0:T(8,128)S(1)} %get-tuple-element.11.refs_2_), custom_call_target="tpu_custom_call" | custom-call | tf_op jit(solution)/shard_map/pallas_call | solution.py:589
Async XLA Ops:
  0.6 0.8 %copy-start = (f32[16384]{0:T(1024)S(1)}, f32[16384]{0:T(1024)}, u32[]{:S(2)}) copy-start(f32[16384]{0:T(1024)} %param.3) | copy-start | bytes 196612
  1.5 0.8 %copy-start.1 = (s32[16384]{0:T(1024)S(1)}, s32[16384]{0:T(1024)}, u32[]{:S(2)}) copy-start(s32[16384]{0:T(1024)} %param.4) | copy-start | bytes 196612

commit v4 on v3

--- a/solution.py
+++ b/solution.py
@@ -172,10 +172,16 @@
     spread_rows(part_b, ((bins % both) // width).astype(jnp.float32))
     tops = local_tops(lw, bins)
     low, high = bins % LANES, bins // LANES
-    own_top = jnp.zeros(lw.shape, jnp.float32)
+    own_tops = []
+    for v in range(rows // 8):
+        at = slice(8 * v, 8 * v + 8)
+        found = jnp.zeros((8, LANES), jnp.float32)
+        for t in range(BINS // LANES):
+            picked = jnp.take_along_axis(jnp.broadcast_to(tops[t:t + 1], (8, LANES)), low[at], axis=1)
+            found = jnp.where(high[at] == t, picked, found)
+        own_tops.append(found)
+    own_top = jnp.concatenate(own_tops, axis=0)
     for t in range(BINS // LANES):
-        picked = jnp.take_along_axis(jnp.broadcast_to(tops[t:t + 1], lw.shape), low, axis=1)
-        own_top = jnp.where(high == t, picked, own_top)
         top_tab[t] = jnp.broadcast_to(tops[t:t + 1], (8, LANES))
     spread_rows(w_b, jnp.exp(lw - own_top))
     load.wait()
@@ -184,16 +190,16 @@
 
     def mask_states(p):
         def step(r, carry):
-            part = part_b[pl.ds(pl.multiple_of(r * 16, 16), 16), :]
-            cols = pl.ds(pl.multiple_of(r * LANES, LANES), LANES)
-            tile = held[:, cols]
-            part_all = jnp.concatenate([part] * (state // 16), axis=0)
-            for k in range(2):
-                at = (2 * p + k) * state
-                ext[at:at + state, cols] = jnp.where(part_all == jnp.bfloat16(k * half + p), tile, zero)
+            for i in range(4):
+                part = part_b[pl.ds(pl.multiple_of((4 * r + i) * 16, 16), 16), :]
+                tile = held[:, pl.ds(pl.multiple_of((4 * r + i) * LANES, LANES), LANES)]
+                part_all = jnp.concatenate([part] * (state // 16), axis=0)
+                for k in range(2):
+                    at = (2 * p + k) * state
+                    ext[4 * r + i, at:at + state] = jnp.where(part_all == jnp.bfloat16(k * half + p), tile, zero)
             return carry
 
-        lax.fori_loop(0, rows, step, 0)
+        lax.fori_loop(0, rows // 4, step, 0)
 
     label = lax.broadcasted_iota(jnp.int32, (width, LANES), 0).astype(jnp.float32).astype(jnp.bfloat16)
 
@@ -208,8 +214,8 @@
             lo_all = jnp.concatenate([lo] * (width // 16), axis=0)
             pieces.append(jnp.where(lo_all == label, w_all, zero))
         spread = jnp.concatenate(pieces, axis=1)
-        cols = pl.ds(pl.multiple_of(c * depth * LANES, LANES), depth * LANES)
-        left = ext[pl.ds(pl.multiple_of(2 * p * state, 2 * state), 2 * state), cols]
+        at = pl.ds(pl.multiple_of(2 * p * state, 2 * state), 2 * state)
+        left = jnp.concatenate([ext[c * depth + j, at] for j in range(depth)], axis=1)
         return lax.dot_general(left, spread, (((1,), (1,)), ((), ())), preferred_element_type=jnp.float32)
 
     def mass_table():
@@ -560,7 +566,7 @@
         out_specs=(vmem, vmem, vmem),
         scratch_shapes=[
             pltpu.VMEM((state, count), jnp.bfloat16),
-            pltpu.VMEM((2 * half * state, count), jnp.bfloat16),
+            pltpu.VMEM((rows, 2 * half * state, LANES), jnp.bfloat16),
             spread(), spread(), spread(), spread(),
             words(BINS // LANES), words(BINS // LANES),
             pltpu.VMEM((2, 2 * state, width), jnp.float32),

time: 44.3 us -> 41.2 us (0.930)
  Pallas kernels: 41.8 us -> 38.7 us
    pallas_call x1, Pallas kernels: 41 us -> 37.9 us  [body(): pl.pallas_call(functools.partial(kernel, groups, float(count * groups)),...]
where the time goes in v4:
time: 41.2 us; the launch traced here: 41 us
  Pallas kernels  38.7 us (94%)
  local copies, waits for them, and re-layouts  1.67 us (4%)
  between operations  0.65 us (2%)
    pallas_call x1, Pallas kernels, body(): pl.pallas_call(functools.partial(kernel, groups, float(count * groups)),...  37.9 us
    unnamed x4, local copies, waits for them, and re-layouts  1.67 us

profile of v4, /device:TPU:0, one launch (start us, length us, event | category | flops | bytes accessed | tf_op | source)
XLA Modules:
  0.0 41.0 jit_solution(12612152356839149516)
XLA Ops:
  0.6 0.0 copy-start
  0.6 0.8 %copy-done = f32[16384]{0:T(1024)S(1)} copy-done((f32[16384]{0:T(1024)S(1)}, f32[16384]{0:T(1024)}, u32[]{:S(2)}) %copy-start) | copy-done | bytes 65560
  1.5 0.0 copy-start.1
  1.5 0.8 %copy-done.1 = s32[16384]{0:T(1024)S(1)} copy-done((s32[16384]{0:T(1024)S(1)}, s32[16384]{0:T(1024)}, u32[]{:S(2)}) %copy-start.1) | copy-done | bytes 65560
  2.3 37.9 %shard_map.58 = (f32[1,512]{1,0:T(1,128)S(1)}, f32[128,512]{1,0:T(8,128)S(1)}, f32[128,128]{1,0:T(8,128)S(1)}) custom-call(f32[128,128]{1,0:T(8,128)S(1)} %bitcast.4, s32[128,128]{1,0:T(8,128)S(1)} %bitcast.5, bf16[128,16384]{1,0:T(8,128)(2,1)} %states_hbm.1), custom_call_target="tpu_custom_call" | custom-call | tf_op jit(solution)/shard_map/pallas_call | solution.py:562
  40.3 0.7 %shard_map.59 = (f32[1,512]{1,0:T(1,128)}, f32[128,512]{1,0:T(8,128)}, f32[128,128]{1,0:T(8,128)}) custom-call(f32[1,512]{1,0:T(1,128)S(1)} %get-tuple-element.9.refs_0_, f32[128,512]{1,0:T(8,128)S(1)} %get-tuple-element.10.refs_1_, f32[128,128]{1,0:T(8,128)S(1)} %get-tuple-element.11.refs_2_), custom_call_target="tpu_custom_call" | custom-call | tf_op jit(solution)/shard_map/pallas_call | solution.py:595
Async XLA Ops:
  0.6 0.8 %copy-start = (f32[16384]{0:T(1024)S(1)}, f32[16384]{0:T(1024)}, u32[]{:S(2)}) copy-start(f32[16384]{0:T(1024)} %param.3) | copy-start | bytes 196612
  1.5 0.8 %copy-start.1 = (s32[16384]{0:T(1024)S(1)}, s32[16384]{0:T(1024)}, u32[]{:S(2)}) copy-start(s32[16384]{0:T(1024)} %param.4) | copy-start | bytes 196612

commit v5 on v4

--- a/solution.py
+++ b/solution.py
@@ -136,9 +136,9 @@
     return value
 
 
-def kernel(groups, whole_count, lw_ref, bins_ref, states_hbm, cum_ref, means_ref, weights_ref,
-           held, ext, lo_b, hi_b, part_b, w_b, top_tab, mass_tab, blocks,
-           tops_send, tops_recv, mass_send, mass_recv, pair_send, pair_recv, by_mine, by_theirs,
+def kernel(groups, whole_count, lw_hbm, bins_hbm, states_hbm, cum_ref, means_ref, weights_ref,
+           lw_ref, bins_ref, held, ext, lo_b, hi_b, part_b, w_b, top_tab, mass_tab, blocks,
+           tops_send, tops_recv, mass_send, mass_recv, pair_recv, by_mine, by_theirs,
            send, recv, send_s, recv_s, fac, stat_send, stat_recv,
            load_sem, table_ss, table_rs, pair_ss, pair_rs, chip_ss, chip_rs, word_ss, word_rs, stat_ss, stat_rs):
     state = held.shape[0]
@@ -158,13 +158,17 @@
     chip, core = me // 2, me % 2
     dests = [pick([o[s] for o in order], chip) for s in range(chips)]
 
-    load = pltpu.make_async_copy(states_hbm, held, load_sem)
-    load.start()
+    loads = [pltpu.make_async_copy(src, dst, load_sem.at[i]) for i, (src, dst) in enumerate(
+        ((bins_hbm, bins_ref), (lw_hbm, lw_ref), (states_hbm, held)))]
+    for load in loads:
+        load.start()
     barrier = pltpu.get_barrier_semaphore()
     for k in range(1, groups):
         pl.semaphore_signal(barrier, inc=1, device_id={"dom": lax.rem(me + k, groups)},
                             device_id_type=pl.DeviceIdType.MESH)
 
+    loads[0].wait()
+    loads[1].wait()
     lw = lw_ref[...]
     bins = bins_ref[...]
     spread_rows(lo_b, (bins % width).astype(jnp.float32))
@@ -172,6 +176,17 @@
     spread_rows(part_b, ((bins % both) // width).astype(jnp.float32))
     tops = local_tops(lw, bins)
     low, high = bins % LANES, bins // LANES
+    loads[2].wait()
+    zero = jnp.zeros((), jnp.bfloat16)
+
+    def mask_tile(r, p):
+        part = part_b[pl.ds(pl.multiple_of(r * 16, 16), 16), :]
+        tile = held[:, pl.ds(pl.multiple_of(r * LANES, LANES), LANES)]
+        part_all = jnp.concatenate([part] * (state // 16), axis=0)
+        for k in range(2):
+            at = (2 * p + k) * state
+            ext[r, at:at + state] = jnp.where(part_all == jnp.bfloat16(k * half + p), tile, zero)
+
     own_tops = []
     for v in range(rows // 8):
         at = slice(8 * v, 8 * v + 8)
@@ -180,23 +195,17 @@
             picked = jnp.take_along_axis(jnp.broadcast_to(tops[t:t + 1], (8, LANES)), low[at], axis=1)
             found = jnp.where(high[at] == t, picked, found)
         own_tops.append(found)
+        for r in range(8 * v, 8 * v + 8):
+            mask_tile(r, 0)
     own_top = jnp.concatenate(own_tops, axis=0)
     for t in range(BINS // LANES):
         top_tab[t] = jnp.broadcast_to(tops[t:t + 1], (8, LANES))
     spread_rows(w_b, jnp.exp(lw - own_top))
-    load.wait()
-
-    zero = jnp.zeros((), jnp.bfloat16)
 
     def mask_states(p):
         def step(r, carry):
             for i in range(4):
-                part = part_b[pl.ds(pl.multiple_of((4 * r + i) * 16, 16), 16), :]
-                tile = held[:, pl.ds(pl.multiple_of((4 * r + i) * LANES, LANES), LANES)]
-                part_all = jnp.concatenate([part] * (state // 16), axis=0)
-                for k in range(2):
-                    at = (2 * p + k) * state
-                    ext[4 * r + i, at:at + state] = jnp.where(part_all == jnp.bfloat16(k * half + p), tile, zero)
+                mask_tile(4 * r + i, p)
             return carry
 
         lax.fori_loop(0, rows // 4, step, 0)
@@ -220,7 +229,7 @@
 
     def mass_table():
         side = 64
-        depth = min(32, rows)
+        depth = min(64, rows)
         per_row = BINS // side
         low_label = lax.broadcasted_iota(jnp.int32, (side, LANES), 0).astype(jnp.float32).astype(jnp.bfloat16)
         turn = lax.broadcasted_iota(jnp.int32, (per_row, LANES), 0)
@@ -266,7 +275,8 @@
         return remote(src, dst, table_ss.at[which], table_rs.at[which], chip, 1 - core)
 
     def pair_copy(u):
-        return remote(pair_send.at[u], pair_recv.at[u], pair_ss.at[u], pair_rs.at[u], chip, 1 - core)
+        theirs = blocks.at[u, pl.ds(pl.multiple_of((1 - core) * state, state), state)]
+        return remote(theirs, pair_recv.at[u], pair_ss.at[u], pair_rs.at[u], chip, 1 - core)
 
     def piece(p):
         return pl.ds(pl.multiple_of(p * per * state, per * state), per * state)
@@ -302,9 +312,6 @@
         return (chip >= first) & (chip <= final)
 
     def give(u):
-        found = blocks[u % 2, pl.ds(pl.multiple_of((1 - core) * state, state), state)]
-        for l in range(per):
-            pair_send[u, l * state:(l + 1) * state] = found[:, l * LANES:(l + 1) * LANES]
         pair_copy(u).start()
 
     def keep(table, s, values):
@@ -358,12 +365,12 @@
             def _(m=m):
                 merge_words(m)
         pair_copy(u).wait_recv()
-        found = blocks[u % 2, pl.ds(pl.multiple_of(core * state, state), state)]
+        found = blocks[u, pl.ds(pl.multiple_of(core * state, state), state)]
         for l in range(per):
             j = p * per + l
             send[s, chunk(j)] = (
                 found[:, l * LANES:(l + 1) * LANES] * by_mine[s * chunks + j, 0:1]
-                + pair_recv[u, l * state:(l + 1) * state] * by_theirs[s * chunks + j, 0:1])
+                + pair_recv[u, :, l * LANES:(l + 1) * LANES] * by_theirs[s * chunks + j, 0:1])
         for m in merging:
             @pl.when((s == m) & merges(m))
             def _(m=m):
@@ -455,7 +462,6 @@
 
     for s in range(chips):
         tops_send[s] = rows_of(top_tab, dests[s], 1 - core)
-    mask_states(0)
     pl.semaphore_wait(barrier, groups - 1)
     table_copy(0).start()
     depth = min(64, rows) if chips <= 4 else min(16, rows)
@@ -464,7 +470,7 @@
     def turn(v, carry):
         u, c = v // steps, v % steps
         s, p = u // half, u % half
-        found = blocks.at[u % 2]
+        found = blocks.at[u]
         added = product(at_step(dests, s), p, c, depth)
 
         found[...] = jnp.where(c > 0, found[...], 0.0) + added
@@ -499,16 +505,17 @@
         return carry
 
     lax.fori_loop(0, units * steps, turn, 0)
-    handle(units - 1)
     close_stats()
-    for c in range(chips):
-        @pl.when(valid(c))
-        def _(c=c):
-            for p in range(half):
+    for p in range(half):
+        if p == half - 1:
+            handle(units - 1)
+        for c in range(chips):
+            @pl.when(valid(c))
+            def _(c=c, p=p):
                 incoming(c, p).wait_recv()
-            for j in range(chunks):
-                at = slice(j * state, (j + 1) * state)
-                send[last, at] = send[last, at] + recv[c, at] * fac[c * chunks + j, 0:1]
+                for j in range(p * per, (p + 1) * per):
+                    at = slice(j * state, (j + 1) * state)
+                    send[last, at] = send[last, at] + recv[c, at] * fac[c * chunks + j, 0:1]
     for j in range(chunks):
         means_ref[:, j * LANES:(j + 1) * LANES] = (send[last, j * state:(j + 1) * state]
                                                    / jnp.maximum(send_s[last, j:j + 1], 1.0))
@@ -562,22 +569,23 @@
     found = pl.pallas_call(
         functools.partial(kernel, groups, float(count * groups)),
         out_shape=shapes,
-        in_specs=[vmem, vmem, hbm],
+        in_specs=[hbm, hbm, hbm],
         out_specs=(vmem, vmem, vmem),
         scratch_shapes=[
+            pltpu.VMEM((rows, LANES), jnp.float32),
+            pltpu.VMEM((rows, LANES), jnp.int32),
             pltpu.VMEM((state, count), jnp.bfloat16),
             pltpu.VMEM((rows, 2 * half * state, LANES), jnp.bfloat16),
             spread(), spread(), spread(), spread(),
             words(BINS // LANES), words(BINS // LANES),
-            pltpu.VMEM((2, 2 * state, width), jnp.float32),
+            pltpu.VMEM((units, 2 * state, width), jnp.float32),
             words(chips, 4), words(chips, 4), words(chips, 4), words(chips, 4),
-            pltpu.VMEM((units, (width // LANES) * state, LANES), jnp.float32),
-            pltpu.VMEM((units, (width // LANES) * state, LANES), jnp.float32),
+            pltpu.VMEM((units, state, width), jnp.float32),
             words(chips * chunks), words(chips * chunks),
             sums(chips), sums(chips + 1), words(chips), words(chips + 1), words((chips + 1) * chunks),
             pltpu.VMEM((8, LANES), jnp.float32),
             words(groups - 1),
-            pltpu.SemaphoreType.DMA,
+            pltpu.SemaphoreType.DMA((3,)),
             pltpu.SemaphoreType.DMA((2,)),
             pltpu.SemaphoreType.DMA((2,)),
             pltpu.SemaphoreType.DMA((units,)),
@@ -591,7 +599,8 @@
         ],
         compiler_params=pltpu.CompilerParams(
             collective_id=0, has_side_effects=True, vmem_limit_bytes=52 * 1024 * 1024),
-    )(log_weights.reshape(rows, LANES), bins.reshape(rows, LANES), states)
+    )(*[pltpu.with_memory_space_constraint(x, pltpu.HBM)
+        for x in (log_weights.reshape(rows, LANES), bins.reshape(rows, LANES), states)])
     cumulative, bin_means, weights = pl.pallas_call(
         drain,
         out_shape=shapes,

time: 41.2 us -> 39.9 us (0.968)
  local copies, waits for them, and re-layouts: 1.67 us -> 0 us
    unnamed x4 -> x0, local copies, waits for them, and re-layouts: 1.67 us -> none
    pallas_call x1, Pallas kernels: 37.9 us -> 38.4 us  [body(): pl.pallas_call(functools.partial(kernel, groups, float(count * groups)),...]
where the time goes in v5:
time: 39.9 us; the launch traced here: 39.8 us
  Pallas kernels  39.1 us (98%)
  between operations  0.64 us (2%)
    pallas_call x1, Pallas kernels, body(): pl.pallas_call(functools.partial(kernel, groups, float(count * groups)),...  38.4 us

profile of v5, /device:TPU:0, one launch (start us, length us, event | category | flops | bytes accessed | tf_op | source)
XLA Modules:
  0.0 39.8 jit_solution(3033378686789823333)
XLA Ops:
  0.6 38.4 %shard_map.58 = (f32[1,512]{1,0:T(1,128)S(1)}, f32[128,512]{1,0:T(8,128)S(1)}, f32[128,128]{1,0:T(8,128)S(1)}) custom-call(f32[128,128]{1,0:T(8,128)} %bitcast.4, s32[128,128]{1,0:T(8,128)} %bitcast.5, bf16[128,16384]{1,0:T(8,128)(2,1)} %states_hbm.1), custom_call_target="tpu_custom_call" | custom-call | tf_op jit(solution)/shard_map/pallas_call | solution.py:569
  39.0 0.7 %shard_map.59 = (f32[1,512]{1,0:T(1,128)}, f32[128,512]{1,0:T(8,128)}, f32[128,128]{1,0:T(8,128)}) custom-call(f32[1,512]{1,0:T(1,128)S(1)} %get-tuple-element.9.refs_0_, f32[128,512]{1,0:T(8,128)S(1)} %get-tuple-element.10.refs_1_, f32[128,128]{1,0:T(8,128)S(1)} %get-tuple-element.11.refs_2_), custom_call_target="tpu_custom_call" | custom-call | tf_op jit(solution)/shard_map/pallas_call | solution.py:604
